TPU v7x, 256 devices: a whole 4x4x8 slice. The times are simulated.
256 devices in a mesh: tm: 16 (over z, core), space: 16 (over x, y).
Axes of the slice: x: 4, y: 4, z: 8, core: 2. Of those that a mesh axis runs over, the one named last changes fastest.
Arguments:
- slab_starts: float32 [16, 4, 4, 4, 128, 128], P('tm', None, None, None, 'space'), may hold values from -1.4 to 6, as said below
- coarse_factor: float32 [4, 128, 128], P(None, 'space'), may hold values from 0.2 to 1
- blend_weight: float32 [128, 128], P('space'), may hold values from 0.2 to 0.9
- blend_flags: int32 [128, 128], P('space'), may hold values 0 or 1
Outputs:
- slab_ends: float32 [16, 4, 4, 4, 128, 128], P('tm', None, None, None, 'space')
- jump_norm: float32 [16], P('tm')
Inputs may be any that keep to these rules, and one draw needn't show every extreme that they name: `slab_starts`: at every node the density and the pressure lie between 0.5 and 2 and each velocity component between -0.7 and 0.7.
All inputs are finite; a program needn't handle non-finite values. No bound on the sum of `blend_flags` on one device may be relied on, other than what follows from the above.
Results may differ from a plain program's by a relative error of at most 0.0003.
Values sent between devices are 32-bit elements; how exact they have to be, the bound alone decides.
No kernel may reach another device: no remote copies, remote signals or barrier semaphores. Data moves between devices by JAX's collectives and lax.ppermute only.
A program may use at most 128 MiB of HBM per device.

v0:
```python
import math

import jax
import jax.numpy as jnp
import numpy as np
from jax import lax
from jax.experimental import pallas as pl
from jax.experimental.pallas import tpu as pltpu
from jax.sharding import Mesh
from jax.sharding import PartitionSpec as P

FSTEPS = 4
SPACE = ("space_0", "space_1")
TM = ("tm_0", "tm_1")
STEP = 0.003
WEIGHTS = (1.0 / 6.0, 5.0 / 6.0, 5.0 / 6.0, 1.0 / 6.0)
ROWS = 32


def derivative_table():
    inner = 1.0 / math.sqrt(5.0)
    points = np.array([-1.0, -inner, inner, 1.0])
    scales = np.array(
        [1.0 / np.prod([points[c] - points[o] for o in range(4) if o != c]) for c in range(4)]
    )
    table = np.zeros((4, 4))
    for r in range(4):
        for c in range(4):
            if r != c:
                table[r, c] = scales[c] / scales[r] / (points[r] - points[c])
        table[r, r] = -np.sum(table[r])
    return table


SPLIT = [[float(2.0 * WEIGHTS[i] * derivative_table()[i, k]) for k in range(4)] for i in range(4)]
SERIES = (105.0 / 52.5, 35.0 / 52.5, 21.0 / 52.5, 15.0 / 52.5)


def log_parts(left, right, log_left, log_right):
    total = left + right
    differ = right - left
    ratio = differ / total
    ratio = ratio * ratio
    nearly = ratio < 0.0001
    series = SERIES[0] + ratio * (SERIES[1] + ratio * (SERIES[2] + ratio * SERIES[3]))
    return jnp.where(nearly, total, differ), jnp.where(nearly, series, log_right - log_left)


def pair_flux(a, b, scale=None):
    top, bottom = log_parts(a["rho"], b["rho"], a["lrho"], b["lrho"])
    mean = top / bottom
    top, bottom = log_parts(a["beta"], b["beta"], a["lbeta"], b["lbeta"])
    thermal = bottom / top
    normal = a["n"] + b["n"]
    pressure = a["p"] + b["p"]
    cross = a["p"] * b["n"] + b["p"] * a["n"]
    if scale is not None:
        mean = mean * scale
        pressure = pressure * scale
        cross = cross * scale
    mass = mean * normal
    half = 0.5 * mass
    kinetic = a["n"] * b["n"] + a["t"] * b["t"] + thermal
    return (
        mass,
        half * normal + pressure,
        half * (a["t"] + b["t"]),
        half * kinetic + cross,
    )


def conserved(node):
    return (node["rho"], node["mn"], node["mt"], node["e"])


def face_flux(a, b):
    central = pair_flux(a, b)
    speed = jnp.maximum(jnp.abs(a["n"]) + a["c"], jnp.abs(b["n"]) + b["c"])
    return tuple(
        c - speed * (ub - ua) for c, ua, ub in zip(central, conserved(a), conserved(b), strict=True)
    )


def physical(node):
    return (
        node["mn"],
        node["mn"] * node["n"] + node["p"],
        node["mt"] * node["n"],
        node["n"] * (node["e"] + node["p"]),
    )


def line_walls(nodes, blend):
    walls = [None, None, None]
    for i in range(4):
        for k in range(i + 1, 4):
            flux = pair_flux(nodes[i], nodes[k], SPLIT[i][k])
            for m in range(i, k):
                walls[m] = (
                    flux
                    if walls[m] is None
                    else tuple(x + y for x, y in zip(walls[m], flux, strict=True))
                )
    own = [physical(node) for node in nodes]
    speeds = [jnp.abs(node["n"]) + node["c"] for node in nodes]
    out = []
    for m in range(3):
        speed = jnp.maximum(speeds[m], speeds[m + 1])
        ua, ub = conserved(nodes[m]), conserved(nodes[m + 1])
        merged = []
        for v in range(4):
            sub = own[m][v] + own[m + 1][v] - speed * (ub[v] - ua[v])
            merged.append(walls[m][v] + blend * (sub - walls[m][v]))
        out.append(merged)
    return out


ORDER = {1: (0, 1, 2, 3), 2: (0, 2, 1, 3)}
VX, VY, PR, LR, BE, LB, CS = range(7)


def at(v, i, j):
    return v * 16 + i * 4 + j


def fine_kernel(
    slab_ref, own_ref, left_ref, right_ref, factor_ref, packed_ref, plain_ref,
    base, mid, blend_ref, prim, faces,
):
    def copy_in(k, carry):
        base[k, 0:8, :] = left_ref[k]
        base[k, 8:16, :] = own_ref[k]
        base[k, 16:24, :] = right_ref[k]
        return carry

    lax.fori_loop(0, 64, copy_in, 0, unroll=8)
    blend_ref[0:8, :] = left_ref[64]
    blend_ref[8:16, :] = own_ref[64]
    blend_ref[16:24, :] = right_ref[64]
    blend_ref[24:32, :] = jnp.zeros((8, 128), jnp.float32)

    def rows(c, offset):
        return pl.ds(pl.multiple_of(c * 8, 8) + offset, 8)

    def node_pass(src, c):
        here = rows(c, 0)
        for n in range(16):
            rho = src[n, here, :]
            inv = 1.0 / rho
            vx = src[16 + n, here, :] * inv
            vy = src[32 + n, here, :] * inv
            p = 0.4 * (src[48 + n, here, :] - 0.5 * rho * (vx * vx + vy * vy))
            beta = 0.2 * rho / p
            prim[VX * 16 + n, here, :] = vx
            prim[VY * 16 + n, here, :] = vy
            prim[PR * 16 + n, here, :] = p
            prim[LR * 16 + n, here, :] = jnp.log(rho)
            prim[BE * 16 + n, here, :] = beta
            prim[LB * 16 + n, here, :] = jnp.log(beta)
            prim[CS * 16 + n, here, :] = jnp.sqrt(1.4 * p * inv)

    def node(src, i, j, here, axis):
        n = i * 4 + j
        normal, along = (VX, VY) if axis == 1 else (VY, VX)
        order = ORDER[axis]
        return {
            "rho": src[n, here, :],
            "mn": src[order[1] * 16 + n, here, :],
            "mt": src[order[2] * 16 + n, here, :],
            "e": src[48 + n, here, :],
            "n": prim[normal * 16 + n, here, :],
            "t": prim[along * 16 + n, here, :],
            "p": prim[PR * 16 + n, here, :],
            "lrho": prim[LR * 16 + n, here, :],
            "beta": prim[BE * 16 + n, here, :],
            "lbeta": prim[LB * 16 + n, here, :],
            "c": prim[CS * 16 + n, here, :],
        }

    def face_pass(src, c):
        for j in range(4):
            flux = face_flux(node(src, 3, j, rows(c, 0), 1), node(src, 0, j, rows(c, 1), 1))
            for v in range(4):
                faces[j * 4 + v, rows(c, 0), :] = flux[v]

    def update_pass(src, dst, c, second):
        here = rows(c, 1)
        blend = blend_ref[rows(c, 0), :]
        share = 0.5 if second else 1.0
        for j in range(4):
            walls = line_walls([node(src, i, j, here, 1) for i in range(4)], blend)
            for v in range(4):
                column = [faces[j * 4 + v, rows(c, 0), :]]
                column += [walls[m][v] for m in range(3)]
                column += [faces[j * 4 + v, here, :]]
                for i in range(4):
                    k = at(v, i, j)
                    change = (share * STEP / WEIGHTS[i]) * (column[i + 1] - column[i])
                    if second:
                        start = 0.5 * (dst[k, rows(c, 2), :] + src[k, here, :])
                    else:
                        start = src[k, here, :]
                    dst[k, rows(c, 0), :] = start - change
        for i in range(4):
            nodes = [node(src, i, j, here, 2) for j in range(4)]
            behind = {key: pltpu.roll(x, 1, 1) for key, x in nodes[3].items()}
            low = face_flux(behind, nodes[0])
            high = tuple(pltpu.roll(x, 127, 1) for x in low)
            walls = line_walls(nodes, blend)
            for q in range(4):
                v = ORDER[2][q]
                column = [low[q]] + [walls[m][q] for m in range(3)] + [high[q]]
                for j in range(4):
                    k = at(v, i, j)
                    change = (share * STEP / WEIGHTS[j]) * (column[j + 1] - column[j])
                    dst[k, rows(c, 0), :] = dst[k, rows(c, 0), :] - change

    def stage(src, dst, s, second):
        for c in range(3):
            blend_ref[8 * c : 8 * c + 8, :] = blend_ref[8 * c + 1 : 8 * c + 9, :]

        def run(body, count):
            def step(c, carry):
                body(c)
                return carry

            lax.fori_loop(0, lax.shift_right_logical(count - 2 * s, 3), step, 0)

        run(lambda c: node_pass(src, c), 31)
        run(lambda c: face_pass(src, c), 30)
        run(lambda c: update_pass(src, dst, c, second), 29)

    def time_step(t, carry):
        stage(base, mid, 2 * t, False)
        stage(mid, base, 2 * t + 1, True)
        return carry

    lax.fori_loop(0, FSTEPS, time_step, 0)

    later = jnp.where(slab_ref[0] == 0, 0.0, 1.0).astype(jnp.float32)
    for v in range(4):
        factor = factor_ref[v]
        mean = weighted_mean([own_ref[v * 16 + n] for n in range(16)])
        for i in range(4):
            kept = []
            for j in range(4):
                k = at(v, i, j)
                guess = mean + factor * (own_ref[k] - mean)
                kept.append(base[k, 0:8, :] - later * guess)
                plain_ref[k] = kept[j]
            for q, piece in enumerate(exchange(kept)):
                packed_ref[v * 4 + q, i] = piece


def weighted_mean(values):
    total = None
    for n, x in enumerate(values):
        term = (WEIGHTS[n // 4] * WEIGHTS[n % 4] / 4.0) * x
        total = term if total is None else total + term
    return total


def exchange(blocks):
    group = lax.broadcasted_iota(jnp.int32, (8, 128), 0) // 2
    out = []
    for q in range(4):
        piece = None
        for j in range(4):
            shift = (2 * (j - q)) % 8
            moved = pltpu.roll(blocks[j], shift, 0) if shift else blocks[j]
            piece = moved if piece is None else jnp.where(group == j, moved, piece)
        out.append(piece)
    return out


def scan_kernel(slab_ref, given_ref, factor_ref, out_ref):
    slab = slab_ref[0]
    var = lax.shift_right_logical(slab, 2)
    first = 2 * (slab & 3)
    row = lax.broadcasted_iota(jnp.int32, (8, 128), 0)
    even = jnp.broadcast_to(factor_ref[var, pl.ds(first, 1), :], (8, 128))
    odd = jnp.broadcast_to(factor_ref[var, pl.ds(first + 1, 1), :], (8, 128))
    factor = jnp.where((row & 1) == 0, even, odd)
    outer = (row < 2) | (row >= 6)
    low = jnp.where(outer, WEIGHTS[0], WEIGHTS[1]).astype(jnp.float32) * (WEIGHTS[0] / 4.0)
    high = jnp.where(outer, WEIGHTS[0], WEIGHTS[1]).astype(jnp.float32) * (WEIGHTS[1] / 4.0)
    state = [given_ref[0, i] for i in range(4)]
    for i in range(4):
        out_ref[0, i] = state[i]
    for n in range(1, 16):
        for i in range(4):
            out_ref[n, i] = state[i]
        if n == 15:
            break
        part = (state[0] + state[3]) * low + (state[1] + state[2]) * high
        part = part + pltpu.roll(part, 4, 0)
        mean = part + pltpu.roll(part, 2, 0)
        state = [mean + factor * (state[i] - mean) + given_ref[n, i] for i in range(4)]


def final_kernel(slab_ref, pieces_ref, opening_ref, plain_ref, factor_ref, end_ref, sum_ref):
    later = jnp.where(slab_ref[0] == 0, 0.0, 1.0).astype(jnp.float32)
    total = jnp.zeros((8, 128), jnp.float32)
    for v in range(4):
        factor = factor_ref[v]
        starts = []
        for i in range(4):
            starts += exchange([pieces_ref[v * 4 + q, i] for q in range(4)])
        mean = weighted_mean(starts)
        squares = []
        for n in range(16):
            k = v * 16 + n
            end_ref[k] = later * (mean + factor * (starts[n] - mean)) + plain_ref[k]
            jump = later * (starts[n] - opening_ref[k])
            squares.append(jump * jump)
        total = total + weighted_mean(squares)
    total = jnp.sum(total, axis=(0, 1), keepdims=True)
    sum_ref[...] = jnp.broadcast_to(total[:, None], sum_ref.shape)


def ring(axis, shift):
    count = lax.axis_size(axis)
    return [(i, (i + shift) % count) for i in range(count)]


def on_device(slab_starts, coarse_factor, blend_weight, blend_flags):
    f32 = jnp.float32
    vmem = pl.BlockSpec(memory_space=pltpu.VMEM)
    smem = pl.BlockSpec(memory_space=pltpu.SMEM)
    opening = slab_starts.reshape(64, 8, 128)
    slab = lax.axis_index(TM).astype(jnp.int32).reshape(1)
    blend = blend_flags.astype(f32) * blend_weight
    own = jnp.concatenate([opening, blend[None]], axis=0)
    left = lax.ppermute(own, SPACE, ring(SPACE, 1))
    right = lax.ppermute(own, SPACE, ring(SPACE, -1))
    packed, plain = pl.pallas_call(
        fine_kernel,
        out_shape=(
            jax.ShapeDtypeStruct((16, 4, 8, 128), f32),
            jax.ShapeDtypeStruct((64, 8, 128), f32),
        ),
        in_specs=[smem] + [vmem] * 4,
        out_specs=[vmem] * 2,
        scratch_shapes=[
            pltpu.VMEM((64, ROWS, 128), f32),
            pltpu.VMEM((64, ROWS, 128), f32),
            pltpu.VMEM((ROWS, 128), f32),
            pltpu.VMEM((7 * 16, ROWS, 128), f32),
            pltpu.VMEM((16, ROWS, 128), f32),
        ],
        name="fine",
    )(slab, own, left, right, coarse_factor)
    gathered = lax.all_to_all(packed, TM, 0, 0)
    scanned = pl.pallas_call(
        scan_kernel,
        out_shape=jax.ShapeDtypeStruct((16, 4, 8, 128), f32),
        in_specs=[smem] + [vmem] * 2,
        out_specs=vmem,
        name="scan",
    )(slab, gathered, coarse_factor)
    starts = lax.all_to_all(scanned, TM, 0, 0)
    slab_end, partial_sums = pl.pallas_call(
        final_kernel,
        out_shape=(
            jax.ShapeDtypeStruct((64, 8, 128), f32),
            jax.ShapeDtypeStruct((16, 1, 128), f32),
        ),
        in_specs=[smem] + [vmem] * 4,
        out_specs=[vmem] * 2,
        name="final",
    )(slab, starts, opening, plain, coarse_factor)
    shared = lax.all_to_all(partial_sums, SPACE, 0, 0)
    element_count = lax.axis_size(SPACE) * slab_starts.shape[4] * slab_starts.shape[5]
    jump_norm = jnp.sqrt(jnp.sum(shared[:, 0, 0]) / element_count)
    return (slab_end.reshape(slab_starts.shape), jump_norm[None])


def solution(mesh):
    split = Mesh(mesh.devices.reshape(8, 2, 4, 4), ("tm_0", "tm_1", "space_0", "space_1"))
    return jax.shard_map(
        on_device,
        mesh=split,
        in_specs=(
            P(TM, None, None, None, SPACE, None),
            P(None, SPACE, None),
            P(SPACE, None),
            P(SPACE, None),
        ),
        out_specs=(P(TM, None, None, None, SPACE, None), P(TM)),
        check_vma=False,
    )
```

profile of v0, /device:TPU:1, one launch (start us, length us, event | category | flops | bytes accessed | tf_op | source)
XLA Modules:
  0.0 90.2 jit_solution(10969145931850953558)
XLA Ops:
  0.6 0.7 multiply_bitcast_fusion
  1.3 1.0 %pad_maximum_fusion.own_ref = f32[65,8,128]{2,1,0:T(8,128)S(1)} fusion(f32[1,8,128]{2,1,0:T(8,128)S(1)} %multiply_bitcast_fusion, f32[64,8,128]{2,1,0:T(8,128)} %bitcast.6), kind=kLoop, calls=%fused_computation | loop fusion | flops 66560 | bytes 532480 | tf_op jit(solution)/shard_map/concatenate | solution.py:333
  2.3 0.0 copy-start
  2.3 5.8 %collective-permute-start.1 = (f32[65,8,128]{2,1,0:T(8,128)S(1)}, f32[65,8,128]{2,1,0:T(8,128)S(1)}, u32[]{:S(2)}, u32[]{:S(2)}) collective-permute-start(f32[65,8,128]{2,1,0:T(8,128)S(1)} %pad_maximum_fusion.own_ref), channel_id=1, source_target_pairs={{0,15},{1,0},{2,1},{3,2},{4,3},{5,4},{6,5},{7,6},{8,7},{9,8},{10,9... | collective-permute-start | bytes 798728 | tf_op jit(solution)/shard_map/ppermute | solution.py:335
  8.1 0.0 collective-permute-start
  8.1 5.1 %collective-permute-done.1.right_ref = f32[65,8,128]{2,1,0:T(8,128)S(1)} collective-permute-done((f32[65,8,128]{2,1,0:T(8,128)S(1)}, f32[65,8,128]{2,1,0:T(8,128)S(1)}, u32[]{:S(2)}, u32[]{:S(2)}) %collective-permute-start.1) | collective-permute-done | bytes 266272 | tf_op jit(solution)/shard_map/ppermute | solution.py:335
  13.2 0.0 copy-start.1
  13.2 5.2 %collective-permute-done.left_ref = f32[65,8,128]{2,1,0:T(8,128)S(1)} collective-permute-done((f32[65,8,128]{2,1,0:T(8,128)S(1)}, f32[65,8,128]{2,1,0:T(8,128)S(1)}, u32[]{:S(2)}, u32[]{:S(2)}) %collective-permute-start) | collective-permute-done | bytes 266272 | tf_op jit(solution)/shard_map/ppermute | solution.py:334
  18.5 0.0 copy-start.2
  18.5 0.0 copy-done
  18.5 0.0 copy-done.1
  18.5 0.7 copy-done.2
  19.2 17.7 %fine.1 = (f32[16,4,8,128]{3,2,1,0:T(8,128)}, f32[64,8,128]{2,1,0:T(8,128)}) custom-call(s32[1]{0:T(128)} %bitcast.slab_ref, f32[65,8,128]{2,1,0:T(8,128)} %copy-done, f32[65,8,128]{2,1,0:T(8,128)} %copy-done.2, f32[65,8,128]{2,1,0:T(8,128)} %copy-done.1, f32[4,8,128]{2,1,0:T(8,128)} %factor_ref.5), custom_call_target="tpu_custom_call" | custom-call | tf_op jit(solution)/shard_map/fine/pallas_call | solution.py:336
  36.8 22.0 %all_to_all.15.given_ref = f32[16,4,8,128]{3,2,1,0:T(8,128)} all-to-all(f32[16,4,8,128]{3,2,1,0:T(8,128)} %get-tuple-element.6), channel_id=1, replica_groups=mesh['tm_0'=8,'tm_1'=2,'space_0'=4,'space_1'=4] {'tm_0','tm_1'}, dimensions={0} | all-to-all | bytes 524288 | tf_op jit(solution)/shard_map/all_to_all | solution.py:353
  58.8 1.8 %scan.1 = f32[16,4,8,128]{3,2,1,0:T(8,128)} custom-call(s32[1]{0:T(128)} %bitcast.slab_ref, f32[16,4,8,128]{3,2,1,0:T(8,128)} %all_to_all.15.given_ref, f32[4,8,128]{2,1,0:T(8,128)} %factor_ref.5), custom_call_target="tpu_custom_call" | custom-call | tf_op jit(solution)/shard_map/scan/pallas_call | solution.py:354
  60.6 15.3 %all_to_all.16.pieces_ref = f32[16,4,8,128]{3,2,1,0:T(8,128)} all-to-all(f32[16,4,8,128]{3,2,1,0:T(8,128)} %scan.1), channel_id=1, replica_groups=mesh['tm_0'=8,'tm_1'=2,'space_0'=4,'space_1'=4] {'tm_0','tm_1'}, dimensions={0} | all-to-all | bytes 524288 | tf_op jit(solution)/shard_map/all_to_all | solution.py:361
  75.9 2.0 %final.1 = (f32[64,8,128]{2,1,0:T(8,128)}, f32[16,1,128]{2,1,0:T(1,128)}) custom-call(s32[1]{0:T(128)} %bitcast.slab_ref, f32[16,4,8,128]{3,2,1,0:T(8,128)} %all_to_all.16.pieces_ref, f32[64,8,128]{2,1,0:T(8,128)} %bitcast.7, f32[64,8,128]{2,1,0:T(8,128)} %get-tuple-element.7.plain_ref, f32[4,8,128]{2,1,0:T(8,128)} %factor_ref.5), custom_call_target="tpu_custom_call" | custom-call | tf_op jit(solution)/shard_map/final/pallas_call | solution.py:362
  77.9 9.8 %all_to_all.17 = f32[16,1,128]{2,1,0:T(1,128)S(1)} all-to-all(f32[16,1,128]{2,1,0:T(1,128)} %get-tuple-element.9), channel_id=1, replica_groups=mesh['tm_0'=8,'tm_1'=2,'space_0'=4,'space_1'=4] {'space_0','space_1'}, dimensions={0} | all-to-all | bytes 16384 | tf_op jit(solution)/shard_map/all_to_all | solution.py:372
  87.7 0.6 slice_reduce_fusion
Async XLA Ops:
  2.3 16.2 %copy-start = (f32[65,8,128]{2,1,0:T(8,128)}, f32[65,8,128]{2,1,0:T(8,128)S(1)}, u32[]{:S(2)}) copy-start(f32[65,8,128]{2,1,0:T(8,128)S(1)} %pad_maximum_fusion.own_ref) | copy-start | bytes 798724
  2.3 10.9 %collective-permute-start.1 = (f32[65,8,128]{2,1,0:T(8,128)S(1)}, f32[65,8,128]{2,1,0:T(8,128)S(1)}, u32[]{:S(2)}, u32[]{:S(2)}) collective-permute-start(f32[65,8,128]{2,1,0:T(8,128)S(1)} %pad_maximum_fusion.own_ref), channel_id=1, source_target_pairs={{0,15},{1,0},{2,1},{3,2},{4,3},{5,4},{6,5},{7,6},{8,7},{9,8},{10,9... | collective-permute-start | bytes 798728 | tf_op jit(solution)/shard_map/ppermute | solution.py:335
  8.1 10.3 %collective-permute-start = (f32[65,8,128]{2,1,0:T(8,128)S(1)}, f32[65,8,128]{2,1,0:T(8,128)S(1)}, u32[]{:S(2)}, u32[]{:S(2)}) collective-permute-start(f32[65,8,128]{2,1,0:T(8,128)S(1)} %pad_maximum_fusion.own_ref), channel_id=1, source_target_pairs={{0,1},{1,2},{2,3},{3,4},{4,5},{5,6},{6,7},{7,8},{8,9},{9,10},{10,1... | collective-permute-start | bytes 798728 | tf_op jit(solution)/shard_map/ppermute | solution.py:334
  13.2 5.2 %copy-start.1 = (f32[65,8,128]{2,1,0:T(8,128)}, f32[65,8,128]{2,1,0:T(8,128)S(1)}, u32[]{:S(2)}) copy-start(f32[65,8,128]{2,1,0:T(8,128)S(1)} %collective-permute-done.1.right_ref) | copy-start | bytes 798724
  18.5 0.7 copy-start.2
where the time goes:
time: 90.7 us; the launch traced here: 90.2 us
  blocking collectives  47.1 us (52%)
  Pallas kernels  21.5 us (24%)
  waiting for transfers between devices  10.3 us (11%)
  starting transfers between devices  5.83 us (6%)
  between operations  2.47 us (3%)
  other arithmetic  2.29 us (3%)
    all_to_all x1, blocking collectives, on_device(): gathered = lax.all_to_all(packed, TM, 0, 0)  22 us
    pallas_call x1, Pallas kernels, on_device(): pl.pallas_call(fine_kernel, out_shape=(jax.ShapeDtypeStruct((16, 4, 8, 12...  17.7 us
    all_to_all x1, blocking collectives, on_device(): starts = lax.all_to_all(scanned, TM, 0, 0)  15.3 us
    all_to_all x1, blocking collectives, on_device(): shared = lax.all_to_all(partial_sums, SPACE, 0, 0)  9.84 us
    ppermute x1, starting transfers between devices, on_device(): right = lax.ppermute(own, SPACE, ring(SPACE, -1))  5.82 us
    ppermute x1, waiting for transfers between devices, on_device(): left = lax.ppermute(own, SPACE, ring(SPACE, 1))  5.24 us
    ppermute x1, waiting for transfers between devices, on_device(): right = lax.ppermute(own, SPACE, ring(SPACE, -1))  5.07 us
    pallas_call x1, Pallas kernels, on_device(): pl.pallas_call(final_kernel, out_shape=(jax.ShapeDtypeStruct((64, 8, 128)...  1.99 us
  transfers between devices with their start and end apart: 2, of which 2 were waited for; matrix products, arithmetic and copies ran while one was open for 0% of the time, Pallas kernels for 0%

commit v1 on v0

--- a/solution.py
+++ b/solution.py
@@ -33,23 +33,27 @@
 
 
 SPLIT = [[float(2.0 * WEIGHTS[i] * derivative_table()[i, k]) for k in range(4)] for i in range(4)]
+EDGE = SPLIT[0][1]
 SERIES = (105.0 / 52.5, 35.0 / 52.5, 21.0 / 52.5, 15.0 / 52.5)
-
-
-def log_parts(left, right, log_left, log_right):
+BINARY = tuple(x / math.log(2.0) for x in SERIES)
+BETA = 0.2 / math.log(2.0)
+SOUND = math.sqrt(1.4 * BETA)
+
+
+def log_parts(left, right, log_left, log_right, terms):
     total = left + right
     differ = right - left
     ratio = differ / total
     ratio = ratio * ratio
     nearly = ratio < 0.0001
-    series = SERIES[0] + ratio * (SERIES[1] + ratio * (SERIES[2] + ratio * SERIES[3]))
+    series = terms[0] + ratio * (terms[1] + ratio * (terms[2] + ratio * terms[3]))
     return jnp.where(nearly, total, differ), jnp.where(nearly, series, log_right - log_left)
 
 
 def pair_flux(a, b, scale=None):
-    top, bottom = log_parts(a["rho"], b["rho"], a["lrho"], b["lrho"])
+    top, bottom = log_parts(a["rho"], b["rho"], a["lrho"], b["lrho"], SERIES)
     mean = top / bottom
-    top, bottom = log_parts(a["beta"], b["beta"], a["lbeta"], b["lbeta"])
+    top, bottom = log_parts(a["beta"], b["beta"], a["lbeta"], b["lbeta"], BINARY)
     thermal = bottom / top
     normal = a["n"] + b["n"]
     pressure = a["p"] + b["p"]
@@ -73,11 +77,11 @@
     return (node["rho"], node["mn"], node["mt"], node["e"])
 
 
-def face_flux(a, b):
+def face_flux(a, b, scale):
     central = pair_flux(a, b)
     speed = jnp.maximum(jnp.abs(a["n"]) + a["c"], jnp.abs(b["n"]) + b["c"])
     return tuple(
-        c - speed * (ub - ua) for c, ua, ub in zip(central, conserved(a), conserved(b), strict=True)
+        scale * (c - speed * (ub - ua)) for c, ua, ub in zip(central, conserved(a), conserved(b), strict=True)
     )
 
 
@@ -90,28 +94,28 @@
     )
 
 
-def line_walls(nodes, blend):
-    walls = [None, None, None]
+def line_walls(nodes, split_share, sub_share):
+    pair = {}
     for i in range(4):
         for k in range(i + 1, 4):
-            flux = pair_flux(nodes[i], nodes[k], SPLIT[i][k])
-            for m in range(i, k):
-                walls[m] = (
-                    flux
-                    if walls[m] is None
-                    else tuple(x + y for x, y in zip(walls[m], flux, strict=True))
-                )
+            scale = None if k - i == 1 and i != 1 else SPLIT[i][k] / EDGE
+            pair[i, k] = pair_flux(nodes[i], nodes[k], scale)
     own = [physical(node) for node in nodes]
     speeds = [jnp.abs(node["n"]) + node["c"] for node in nodes]
-    out = []
-    for m in range(3):
-        speed = jnp.maximum(speeds[m], speeds[m + 1])
-        ua, ub = conserved(nodes[m]), conserved(nodes[m + 1])
-        merged = []
-        for v in range(4):
-            sub = own[m][v] + own[m + 1][v] - speed * (ub[v] - ua[v])
-            merged.append(walls[m][v] + blend * (sub - walls[m][v]))
-        out.append(merged)
+    out = [[], [], []]
+    for v in range(4):
+        far = pair[0, 3][v]
+        left, right = far + pair[0, 2][v], far + pair[1, 3][v]
+        walls = (
+            left + pair[0, 1][v],
+            (left + pair[1, 3][v]) + pair[1, 2][v],
+            right + pair[2, 3][v],
+        )
+        for m in range(3):
+            speed = jnp.maximum(speeds[m], speeds[m + 1])
+            jump = conserved(nodes[m + 1])[v] - conserved(nodes[m])[v]
+            sub = own[m][v] + own[m + 1][v] - speed * jump
+            out[m].append(split_share * walls[m] + sub_share * sub)
     return out
 
 
@@ -134,9 +138,9 @@
         return carry
 
     lax.fori_loop(0, 64, copy_in, 0, unroll=8)
-    blend_ref[0:8, :] = left_ref[64]
-    blend_ref[8:16, :] = own_ref[64]
-    blend_ref[16:24, :] = right_ref[64]
+    blend_ref[0:8, :] = left_ref[64] * left_ref[65]
+    blend_ref[8:16, :] = own_ref[64] * own_ref[65]
+    blend_ref[16:24, :] = right_ref[64] * right_ref[65]
     blend_ref[24:32, :] = jnp.zeros((8, 128), jnp.float32)
 
     def rows(c, offset):
@@ -147,17 +151,19 @@
         for n in range(16):
             rho = src[n, here, :]
             inv = 1.0 / rho
-            vx = src[16 + n, here, :] * inv
-            vy = src[32 + n, here, :] * inv
-            p = 0.4 * (src[48 + n, here, :] - 0.5 * rho * (vx * vx + vy * vy))
-            beta = 0.2 * rho / p
+            mx = src[16 + n, here, :]
+            my = src[32 + n, here, :]
+            vx = mx * inv
+            vy = my * inv
+            p = 0.4 * src[48 + n, here, :] - 0.2 * (mx * vx + my * vy)
+            beta = BETA * rho / p
             prim[VX * 16 + n, here, :] = vx
             prim[VY * 16 + n, here, :] = vy
             prim[PR * 16 + n, here, :] = p
             prim[LR * 16 + n, here, :] = jnp.log(rho)
             prim[BE * 16 + n, here, :] = beta
-            prim[LB * 16 + n, here, :] = jnp.log(beta)
-            prim[CS * 16 + n, here, :] = jnp.sqrt(1.4 * p * inv)
+            prim[LB * 16 + n, here, :] = jnp.log2(beta)
+            prim[CS * 16 + n, here, :] = SOUND * lax.rsqrt(beta)
 
     def node(src, i, j, here, axis):
         n = i * 4 + j
@@ -177,25 +183,31 @@
             "c": prim[CS * 16 + n, here, :],
         }
 
-    def face_pass(src, c):
+    def face_pass(src, c, scale):
         for j in range(4):
-            flux = face_flux(node(src, 3, j, rows(c, 0), 1), node(src, 0, j, rows(c, 1), 1))
+            flux = face_flux(node(src, 3, j, rows(c, 0), 1), node(src, 0, j, rows(c, 1), 1), scale)
             for v in range(4):
                 faces[j * 4 + v, rows(c, 0), :] = flux[v]
 
     def update_pass(src, dst, c, second):
         here = rows(c, 1)
         blend = blend_ref[rows(c, 0), :]
-        share = 0.5 if second else 1.0
+        scale = (0.5 if second else 1.0) * STEP / WEIGHTS[1]
+        sub_share = scale * blend
+        split_share = (scale - sub_share) * EDGE
         for j in range(4):
-            walls = line_walls([node(src, i, j, here, 1) for i in range(4)], blend)
+            walls = line_walls(
+                [node(src, i, j, here, 1) for i in range(4)], split_share, sub_share
+            )
             for v in range(4):
                 column = [faces[j * 4 + v, rows(c, 0), :]]
                 column += [walls[m][v] for m in range(3)]
                 column += [faces[j * 4 + v, here, :]]
                 for i in range(4):
                     k = at(v, i, j)
-                    change = (share * STEP / WEIGHTS[i]) * (column[i + 1] - column[i])
+                    change = column[i + 1] - column[i]
+                    if i in (0, 3):
+                        change = (WEIGHTS[1] / WEIGHTS[0]) * change
                     if second:
                         start = 0.5 * (dst[k, rows(c, 2), :] + src[k, here, :])
                     else:
@@ -204,15 +216,17 @@
         for i in range(4):
             nodes = [node(src, i, j, here, 2) for j in range(4)]
             behind = {key: pltpu.roll(x, 1, 1) for key, x in nodes[3].items()}
-            low = face_flux(behind, nodes[0])
+            low = face_flux(behind, nodes[0], scale)
             high = tuple(pltpu.roll(x, 127, 1) for x in low)
-            walls = line_walls(nodes, blend)
+            walls = line_walls(nodes, split_share, sub_share)
             for q in range(4):
                 v = ORDER[2][q]
                 column = [low[q]] + [walls[m][q] for m in range(3)] + [high[q]]
                 for j in range(4):
                     k = at(v, i, j)
-                    change = (share * STEP / WEIGHTS[j]) * (column[j + 1] - column[j])
+                    change = column[j + 1] - column[j]
+                    if j in (0, 3):
+                        change = (WEIGHTS[1] / WEIGHTS[0]) * change
                     dst[k, rows(c, 0), :] = dst[k, rows(c, 0), :] - change
 
     def stage(src, dst, s, second):
@@ -227,7 +241,8 @@
             lax.fori_loop(0, lax.shift_right_logical(count - 2 * s, 3), step, 0)
 
         run(lambda c: node_pass(src, c), 31)
-        run(lambda c: face_pass(src, c), 30)
+        scale = (0.5 if second else 1.0) * STEP / WEIGHTS[1]
+        run(lambda c: face_pass(src, c, scale), 30)
         run(lambda c: update_pass(src, dst, c, second), 29)
 
     def time_step(t, carry):
@@ -318,6 +333,10 @@
     sum_ref[...] = jnp.broadcast_to(total[:, None], sum_ref.shape)
 
 
+def hold(x):
+    return pltpu.with_memory_space_constraint(x, pltpu.VMEM)
+
+
 def ring(axis, shift):
     count = lax.axis_size(axis)
     return [(i, (i + shift) % count) for i in range(count)]
@@ -329,15 +348,14 @@
     smem = pl.BlockSpec(memory_space=pltpu.SMEM)
     opening = slab_starts.reshape(64, 8, 128)
     slab = lax.axis_index(TM).astype(jnp.int32).reshape(1)
-    blend = blend_flags.astype(f32) * blend_weight
-    own = jnp.concatenate([opening, blend[None]], axis=0)
+    own = jnp.concatenate([opening, blend_weight[None], blend_flags[None].astype(f32)], axis=0)
     left = lax.ppermute(own, SPACE, ring(SPACE, 1))
     right = lax.ppermute(own, SPACE, ring(SPACE, -1))
     packed, plain = pl.pallas_call(
         fine_kernel,
         out_shape=(
-            jax.ShapeDtypeStruct((16, 4, 8, 128), f32),
-            jax.ShapeDtypeStruct((64, 8, 128), f32),
+            pltpu.VMEM((16, 4, 8, 128), f32),
+            pltpu.VMEM((64, 8, 128), f32),
         ),
         in_specs=[smem] + [vmem] * 4,
         out_specs=[vmem] * 2,
@@ -349,26 +367,26 @@
             pltpu.VMEM((16, ROWS, 128), f32),
         ],
         name="fine",
-    )(slab, own, left, right, coarse_factor)
+    )(slab, hold(own), hold(left), hold(right), coarse_factor)
     gathered = lax.all_to_all(packed, TM, 0, 0)
     scanned = pl.pallas_call(
         scan_kernel,
-        out_shape=jax.ShapeDtypeStruct((16, 4, 8, 128), f32),
+        out_shape=pltpu.VMEM((16, 4, 8, 128), f32),
         in_specs=[smem] + [vmem] * 2,
         out_specs=vmem,
         name="scan",
-    )(slab, gathered, coarse_factor)
+    )(slab, hold(gathered), coarse_factor)
     starts = lax.all_to_all(scanned, TM, 0, 0)
     slab_end, partial_sums = pl.pallas_call(
         final_kernel,
         out_shape=(
             jax.ShapeDtypeStruct((64, 8, 128), f32),
-            jax.ShapeDtypeStruct((16, 1, 128), f32),
+            pltpu.VMEM((16, 1, 128), f32),
         ),
         in_specs=[smem] + [vmem] * 4,
         out_specs=[vmem] * 2,
         name="final",
-    )(slab, starts, opening, plain, coarse_factor)
+    )(slab, hold(starts), opening, hold(plain), coarse_factor)
     shared = lax.all_to_all(partial_sums, SPACE, 0, 0)
     element_count = lax.axis_size(SPACE) * slab_starts.shape[4] * slab_starts.shape[5]
     jump_norm = jnp.sqrt(jnp.sum(shared[:, 0, 0]) / element_count)

time: 90.7 us -> 85.6 us (0.944)
  Pallas kernels: 21.5 us -> 19.1 us
  blocking collectives: 47.1 us -> 45 us
    pallas_call x2, Pallas kernels: 19.5 us -> 17.3 us  [the longest x1 16.5 us: on_device(): pl.pallas_call(fine_kernel, out_shape=(pltpu.VMEM((16, 4, 8, 128), f32),...]
    all_to_all x1, blocking collectives: 15.3 us -> 14.4 us  [on_device(): starts = lax.all_to_all(scanned, TM, 0, 0)]
where the time goes in v1:
time: 85.6 us; the launch traced here: 85.1 us
  blocking collectives  45 us (53%)
  Pallas kernels  19.1 us (22%)
  waiting for transfers between devices  10.4 us (12%)
  starting transfers between devices  5.83 us (7%)
  between operations  2.47 us (3%)
  other arithmetic  2.28 us (3%)
    all_to_all x1, blocking collectives, on_device(): gathered = lax.all_to_all(packed, TM, 0, 0)  21.7 us
    pallas_call x1, Pallas kernels, on_device(): pl.pallas_call(fine_kernel, out_shape=(pltpu.VMEM((16, 4, 8, 128), f32),...  16.5 us
    all_to_all x1, blocking collectives, on_device(): starts = lax.all_to_all(scanned, TM, 0, 0)  14.4 us
    all_to_all x1, blocking collectives, on_device(): shared = lax.all_to_all(partial_sums, SPACE, 0, 0)  8.97 us
    ppermute x1, starting transfers between devices, on_device(): right = lax.ppermute(own, SPACE, ring(SPACE, -1))  5.82 us
    ppermute x1, waiting for transfers between devices, on_device(): left = lax.ppermute(own, SPACE, ring(SPACE, 1))  5.24 us
    ppermute x1, waiting for transfers between devices, on_device(): right = lax.ppermute(own, SPACE, ring(SPACE, -1))  5.16 us
    pallas_call x1, Pallas kernels, on_device(): pl.pallas_call(final_kernel, out_shape=(jax.ShapeDtypeStruct((64, 8, 128)...  1.81 us
  transfers between devices with their start and end apart: 2, of which 2 were waited for; matrix products, arithmetic and copies ran while one was open for 0% of the time, Pallas kernels for 0%

profile of v1, /device:TPU:1, one launch (start us, length us, event | category | flops | bytes accessed | tf_op | source)
XLA Modules:
  0.0 85.1 jit_solution(854077927419785296)
XLA Ops:
  0.6 0.0 copy-start
  0.6 0.7 convert_bitcast_fusion
  1.3 0.0 copy-done
  1.3 1.0 %pad_maximum_fusion.own_ref = f32[66,8,128]{2,1,0:T(8,128)S(1)} fusion(f32[1,8,128]{2,1,0:T(8,128)S(1)} %convert_bitcast_fusion, f32[1,8,128]{2,1,0:T(8,128)S(1)} %bitcast.9, f32[64,8,128]{2,1,0:T(8,128)} %bitcast.7), kind=kLoop, calls=%fused_computation | loop fusion | flops 135168 | bytes 540672 | tf_op jit(solution)/shard_map/concatenate | solution.py:351
  2.3 5.8 %collective-permute-start.1 = (f32[66,8,128]{2,1,0:T(8,128)S(1)}, f32[66,8,128]{2,1,0:T(8,128)S(1)}, u32[]{:S(2)}, u32[]{:S(2)}) collective-permute-start(f32[66,8,128]{2,1,0:T(8,128)S(1)} %pad_maximum_fusion.own_ref), channel_id=1, source_target_pairs={{0,15},{1,0},{2,1},{3,2},{4,3},{5,4},{6,5},{7,6},{8,7},{9,8},{10,9... | collective-permute-start | bytes 811016 | tf_op jit(solution)/shard_map/ppermute | solution.py:353
  8.1 0.0 collective-permute-start
  8.1 5.2 %collective-permute-done.1.right_ref = f32[66,8,128]{2,1,0:T(8,128)S(1)} collective-permute-done((f32[66,8,128]{2,1,0:T(8,128)S(1)}, f32[66,8,128]{2,1,0:T(8,128)S(1)}, u32[]{:S(2)}, u32[]{:S(2)}) %collective-permute-start.1) | collective-permute-done | bytes 270368 | tf_op jit(solution)/shard_map/ppermute | solution.py:353
  13.3 5.2 %collective-permute-done.left_ref = f32[66,8,128]{2,1,0:T(8,128)S(1)} collective-permute-done((f32[66,8,128]{2,1,0:T(8,128)S(1)}, f32[66,8,128]{2,1,0:T(8,128)S(1)}, u32[]{:S(2)}, u32[]{:S(2)}) %collective-permute-start) | collective-permute-done | bytes 270368 | tf_op jit(solution)/shard_map/ppermute | solution.py:352
  18.5 16.5 %fine.1 = (f32[16,4,8,128]{3,2,1,0:T(8,128)S(1)}, f32[64,8,128]{2,1,0:T(8,128)S(1)}) custom-call(s32[1]{0:T(128)} %bitcast.slab_ref, f32[66,8,128]{2,1,0:T(8,128)S(1)} %pad_maximum_fusion.own_ref, f32[66,8,128]{2,1,0:T(8,128)S(1)} %collective-permute-done.left_ref, f32[66,8,128]{2,1,0:T(8,128)S(1)} %collective-permute-done.1.right_ref, f32[4,8,128]{2,1,0:T(8,128)} %factor_ref.5), custom_call_target="tpu_custom_call" | custom-call | tf_op jit(solution)/shard_map/fine/pallas_call | solution.py:354
  35.0 21.7 %all_to_all.15.given_ref = f32[16,4,8,128]{3,2,1,0:T(8,128)S(1)} all-to-all(f32[16,4,8,128]{3,2,1,0:T(8,128)S(1)} %get-tuple-element.6), channel_id=1, replica_groups=mesh['tm_0'=8,'tm_1'=2,'space_0'=4,'space_1'=4] {'tm_0','tm_1'}, dimensions={0} | all-to-all | bytes 524288 | tf_op jit(solution)/shard_map/all_to_all | solution.py:371
  56.7 0.9 %scan.1 = f32[16,4,8,128]{3,2,1,0:T(8,128)S(1)} custom-call(s32[1]{0:T(128)} %bitcast.slab_ref, f32[16,4,8,128]{3,2,1,0:T(8,128)S(1)} %all_to_all.15.given_ref, f32[4,8,128]{2,1,0:T(8,128)} %factor_ref.5), custom_call_target="tpu_custom_call" | custom-call | tf_op jit(solution)/shard_map/scan/pallas_call | solution.py:372
  57.6 14.4 %all_to_all.16.pieces_ref = f32[16,4,8,128]{3,2,1,0:T(8,128)S(1)} all-to-all(f32[16,4,8,128]{3,2,1,0:T(8,128)S(1)} %scan.1), channel_id=1, replica_groups=mesh['tm_0'=8,'tm_1'=2,'space_0'=4,'space_1'=4] {'tm_0','tm_1'}, dimensions={0} | all-to-all | bytes 524288 | tf_op jit(solution)/shard_map/all_to_all | solution.py:379
  71.9 1.8 %final.1 = (f32[64,8,128]{2,1,0:T(8,128)}, f32[16,1,128]{2,1,0:T(1,128)S(1)}) custom-call(s32[1]{0:T(128)} %bitcast.slab_ref, f32[16,4,8,128]{3,2,1,0:T(8,128)S(1)} %all_to_all.16.pieces_ref, f32[64,8,128]{2,1,0:T(8,128)} %bitcast.8, f32[64,8,128]{2,1,0:T(8,128)S(1)} %get-tuple-element.7.plain_ref, f32[4,8,128]{2,1,0:T(8,128)} %factor_ref.5), custom_call_target="tpu_custom_call" | custom-call | tf_op jit(solution)/shard_map/final/pallas_call | solution.py:380
  73.7 9.0 %all_to_all.17 = f32[16,1,128]{2,1,0:T(1,128)S(1)} all-to-all(f32[16,1,128]{2,1,0:T(1,128)S(1)} %get-tuple-element.9), channel_id=1, replica_groups=mesh['tm_0'=8,'tm_1'=2,'space_0'=4,'space_1'=4] {'space_0','space_1'}, dimensions={0} | all-to-all | bytes 16384 | tf_op jit(solution)/shard_map/all_to_all | solution.py:390
  82.7 0.6 slice_reduce_fusion
Async XLA Ops:
  0.6 0.7 copy-start
  2.3 11.0 %collective-permute-start.1 = (f32[66,8,128]{2,1,0:T(8,128)S(1)}, f32[66,8,128]{2,1,0:T(8,128)S(1)}, u32[]{:S(2)}, u32[]{:S(2)}) collective-permute-start(f32[66,8,128]{2,1,0:T(8,128)S(1)} %pad_maximum_fusion.own_ref), channel_id=1, source_target_pairs={{0,15},{1,0},{2,1},{3,2},{4,3},{5,4},{6,5},{7,6},{8,7},{9,8},{10,9... | collective-permute-start | bytes 811016 | tf_op jit(solution)/shard_map/ppermute | solution.py:353
  8.1 10.4 %collective-permute-start = (f32[66,8,128]{2,1,0:T(8,128)S(1)}, f32[66,8,128]{2,1,0:T(8,128)S(1)}, u32[]{:S(2)}, u32[]{:S(2)}) collective-permute-start(f32[66,8,128]{2,1,0:T(8,128)S(1)} %pad_maximum_fusion.own_ref), channel_id=1, source_target_pairs={{0,1},{1,2},{2,3},{3,4},{4,5},{5,6},{6,7},{7,8},{8,9},{9,10},{10,1... | collective-permute-start | bytes 811016 | tf_op jit(solution)/shard_map/ppermute | solution.py:352

commit v2 on v1

--- a/solution.py
+++ b/solution.py
@@ -14,7 +14,6 @@
 TM = ("tm_0", "tm_1")
 STEP = 0.003
 WEIGHTS = (1.0 / 6.0, 5.0 / 6.0, 5.0 / 6.0, 1.0 / 6.0)
-ROWS = 32
 
 
 def derivative_table():
@@ -127,127 +126,199 @@
     return v * 16 + i * 4 + j
 
 
+def rows(c, offset):
+    start = c * 8 + offset
+    if isinstance(c, int):
+        return pl.ds(start, 8)
+    return pl.ds(pl.multiple_of(c * 8, 8) + offset, 8)
+
+
+def node_pass(src, prim, c):
+    here = rows(c, 0)
+    for n in range(16):
+        rho = src[n, here, :]
+        inv = 1.0 / rho
+        mx = src[16 + n, here, :]
+        my = src[32 + n, here, :]
+        vx = mx * inv
+        vy = my * inv
+        p = 0.4 * src[48 + n, here, :] - 0.2 * (mx * vx + my * vy)
+        beta = BETA * rho / p
+        prim[VX * 16 + n, here, :] = vx
+        prim[VY * 16 + n, here, :] = vy
+        prim[PR * 16 + n, here, :] = p
+        prim[LR * 16 + n, here, :] = jnp.log(rho)
+        prim[BE * 16 + n, here, :] = beta
+        prim[LB * 16 + n, here, :] = jnp.log2(beta)
+        prim[CS * 16 + n, here, :] = SOUND * lax.rsqrt(beta)
+
+
+def node(src, prim, i, j, here, axis):
+    n = i * 4 + j
+    normal, along = (VX, VY) if axis == 1 else (VY, VX)
+    order = ORDER[axis]
+    return {
+        "rho": src[n, here, :],
+        "mn": src[order[1] * 16 + n, here, :],
+        "mt": src[order[2] * 16 + n, here, :],
+        "e": src[48 + n, here, :],
+        "n": prim[normal * 16 + n, here, :],
+        "t": prim[along * 16 + n, here, :],
+        "p": prim[PR * 16 + n, here, :],
+        "lrho": prim[LR * 16 + n, here, :],
+        "beta": prim[BE * 16 + n, here, :],
+        "lbeta": prim[LB * 16 + n, here, :],
+        "c": prim[CS * 16 + n, here, :],
+    }
+
+
+def face_pass(src, prim, faces, c, scale):
+    for j in range(4):
+        lower = node(src, prim, 3, j, rows(c, 0), 1)
+        flux = face_flux(lower, node(src, prim, 0, j, rows(c, 1), 1), scale)
+        for v in range(4):
+            faces[j * 4 + v, rows(c, 0), :] = flux[v]
+
+
+def update_pass(src, dst, prim, faces, c, blend, second, right):
+    here = rows(c, 1)
+    there, start_rows = (rows(c, 2), rows(c, 0)) if right else (rows(c, 0), rows(c, 2))
+    scale = (0.5 if second else 1.0) * STEP / WEIGHTS[1]
+    sub_share = scale * blend
+    split_share = (scale - sub_share) * EDGE
+    for j in range(4):
+        nodes = [node(src, prim, i, j, here, 1) for i in range(4)]
+        walls = line_walls(nodes, split_share, sub_share)
+        for v in range(4):
+            column = [faces[j * 4 + v, rows(c, 0), :]]
+            column += [walls[m][v] for m in range(3)]
+            column += [faces[j * 4 + v, here, :]]
+            for i in range(4):
+                k = at(v, i, j)
+                change = column[i + 1] - column[i]
+                if i in (0, 3):
+                    change = (WEIGHTS[1] / WEIGHTS[0]) * change
+                if second:
+                    start = 0.5 * (dst[k, start_rows, :] + src[k, here, :])
+                else:
+                    start = src[k, here, :]
+                dst[k, there, :] = start - change
+    for i in range(4):
+        nodes = [node(src, prim, i, j, here, 2) for j in range(4)]
+        behind = {key: pltpu.roll(x, 1, 1) for key, x in nodes[3].items()}
+        low = face_flux(behind, nodes[0], scale)
+        high = tuple(pltpu.roll(x, 127, 1) for x in low)
+        walls = line_walls(nodes, split_share, sub_share)
+        for q in range(4):
+            v = ORDER[2][q]
+            column = [low[q]] + [walls[m][q] for m in range(3)] + [high[q]]
+            for j in range(4):
+                k = at(v, i, j)
+                change = column[j + 1] - column[j]
+                if j in (0, 3):
+                    change = (WEIGHTS[1] / WEIGHTS[0]) * change
+                dst[k, there, :] = dst[k, there, :] - change
+
+
+def loop(count, body):
+    if isinstance(count, int) and count == 1:
+        body(0)
+        return
+
+    def step(c, carry):
+        body(c)
+        return carry
+
+    lax.fori_loop(0, count, step, 0)
+
+
+def stage(src, dst, work, second, right, chunks, blend_at, updates):
+    prim, faces = work
+    scale = (0.5 if second else 1.0) * STEP / WEIGHTS[1]
+    loop(chunks, lambda c: node_pass(src, prim, c))
+    loop(chunks, lambda c: face_pass(src, prim, faces, c, scale))
+    loop(
+        updates, lambda c: update_pass(src, dst, prim, faces, c, blend_at(c), second, right)
+    )
+
+
+def inner_kernel(own_ref, inner_ref, base, mid, prim, faces):
+    for k in range(64):
+        base[k, 0:8, :] = own_ref[k]
+    blend = own_ref[64] * own_ref[65]
+    for s in range(1, 4):
+        second = s == 2
+        src, dst = (mid, base) if second else (base, mid)
+        shifted = pltpu.roll(blend, 8 - s, 0)
+        stage(src, dst, (prim, faces), second, False, 1, lambda c: shifted, 1)
+        for k in range(64):
+            inner_ref[s - 1, k] = dst[k, 0:8, :]
+
+
+def right_kernel(own_ref, right_ref, inner_ref, out_ref, base, mid, prim, faces, blend_ref):
+    for k in range(64):
+        base[k, 0:2, :] = own_ref[k, 6:8, :]
+        base[k, 2:10, :] = right_ref[k]
+    blend_ref[0:8, :] = own_ref[64] * own_ref[65]
+    blend_ref[8:16, :] = right_ref[64] * right_ref[65]
+
+    def fill(dst, s):
+        def one(k, carry):
+            dst[k, 0:2, :] = inner_ref[s - 1, k, pl.ds(6 - 2 * s, 2), :]
+            return carry
+
+        lax.fori_loop(0, 64, one, 0, unroll=16)
+
+    def time_step(t, carry):
+        for second in (False, True):
+            s = 2 * t + (2 if second else 1)
+            src, dst = (mid, base) if second else (base, mid)
+            blend_at = lambda c, s=s: blend_ref[pl.ds(8 - s, 8), :]
+            stage(src, dst, (prim, faces), second, True, 2, blend_at, 1)
+            fill(dst, jnp.minimum(s, 3))
+        return carry
+
+    lax.fori_loop(0, 2, time_step, 0)
+    for k in range(64):
+        out_ref[k] = base[k, 2:10, :]
+
+
 def fine_kernel(
-    slab_ref, own_ref, left_ref, right_ref, factor_ref, packed_ref, plain_ref,
-    base, mid, blend_ref, prim, faces,
+    slab_ref, own_ref, left_ref, right_ref, inner_ref, strip_ref, factor_ref,
+    packed_ref, plain_ref, base, mid, prim, faces, blend_ref,
 ):
-    def copy_in(k, carry):
+    for k in range(64):
         base[k, 0:8, :] = left_ref[k]
-        base[k, 8:16, :] = own_ref[k]
-        base[k, 16:24, :] = right_ref[k]
-        return carry
-
-    lax.fori_loop(0, 64, copy_in, 0, unroll=8)
+        base[k, 8:10, :] = own_ref[k, 0:2, :]
     blend_ref[0:8, :] = left_ref[64] * left_ref[65]
     blend_ref[8:16, :] = own_ref[64] * own_ref[65]
     blend_ref[16:24, :] = right_ref[64] * right_ref[65]
-    blend_ref[24:32, :] = jnp.zeros((8, 128), jnp.float32)
-
-    def rows(c, offset):
-        return pl.ds(pl.multiple_of(c * 8, 8) + offset, 8)
-
-    def node_pass(src, c):
-        here = rows(c, 0)
-        for n in range(16):
-            rho = src[n, here, :]
-            inv = 1.0 / rho
-            mx = src[16 + n, here, :]
-            my = src[32 + n, here, :]
-            vx = mx * inv
-            vy = my * inv
-            p = 0.4 * src[48 + n, here, :] - 0.2 * (mx * vx + my * vy)
-            beta = BETA * rho / p
-            prim[VX * 16 + n, here, :] = vx
-            prim[VY * 16 + n, here, :] = vy
-            prim[PR * 16 + n, here, :] = p
-            prim[LR * 16 + n, here, :] = jnp.log(rho)
-            prim[BE * 16 + n, here, :] = beta
-            prim[LB * 16 + n, here, :] = jnp.log2(beta)
-            prim[CS * 16 + n, here, :] = SOUND * lax.rsqrt(beta)
-
-    def node(src, i, j, here, axis):
-        n = i * 4 + j
-        normal, along = (VX, VY) if axis == 1 else (VY, VX)
-        order = ORDER[axis]
-        return {
-            "rho": src[n, here, :],
-            "mn": src[order[1] * 16 + n, here, :],
-            "mt": src[order[2] * 16 + n, here, :],
-            "e": src[48 + n, here, :],
-            "n": prim[normal * 16 + n, here, :],
-            "t": prim[along * 16 + n, here, :],
-            "p": prim[PR * 16 + n, here, :],
-            "lrho": prim[LR * 16 + n, here, :],
-            "beta": prim[BE * 16 + n, here, :],
-            "lbeta": prim[LB * 16 + n, here, :],
-            "c": prim[CS * 16 + n, here, :],
-        }
-
-    def face_pass(src, c, scale):
-        for j in range(4):
-            flux = face_flux(node(src, 3, j, rows(c, 0), 1), node(src, 0, j, rows(c, 1), 1), scale)
-            for v in range(4):
-                faces[j * 4 + v, rows(c, 0), :] = flux[v]
-
-    def update_pass(src, dst, c, second):
-        here = rows(c, 1)
-        blend = blend_ref[rows(c, 0), :]
-        scale = (0.5 if second else 1.0) * STEP / WEIGHTS[1]
-        sub_share = scale * blend
-        split_share = (scale - sub_share) * EDGE
-        for j in range(4):
-            walls = line_walls(
-                [node(src, i, j, here, 1) for i in range(4)], split_share, sub_share
-            )
-            for v in range(4):
-                column = [faces[j * 4 + v, rows(c, 0), :]]
-                column += [walls[m][v] for m in range(3)]
-                column += [faces[j * 4 + v, here, :]]
-                for i in range(4):
-                    k = at(v, i, j)
-                    change = column[i + 1] - column[i]
-                    if i in (0, 3):
-                        change = (WEIGHTS[1] / WEIGHTS[0]) * change
-                    if second:
-                        start = 0.5 * (dst[k, rows(c, 2), :] + src[k, here, :])
-                    else:
-                        start = src[k, here, :]
-                    dst[k, rows(c, 0), :] = start - change
-        for i in range(4):
-            nodes = [node(src, i, j, here, 2) for j in range(4)]
-            behind = {key: pltpu.roll(x, 1, 1) for key, x in nodes[3].items()}
-            low = face_flux(behind, nodes[0], scale)
-            high = tuple(pltpu.roll(x, 127, 1) for x in low)
-            walls = line_walls(nodes, split_share, sub_share)
-            for q in range(4):
-                v = ORDER[2][q]
-                column = [low[q]] + [walls[m][q] for m in range(3)] + [high[q]]
-                for j in range(4):
-                    k = at(v, i, j)
-                    change = column[j + 1] - column[j]
-                    if j in (0, 3):
-                        change = (WEIGHTS[1] / WEIGHTS[0]) * change
-                    dst[k, rows(c, 0), :] = dst[k, rows(c, 0), :] - change
-
-    def stage(src, dst, s, second):
-        for c in range(3):
-            blend_ref[8 * c : 8 * c + 8, :] = blend_ref[8 * c + 1 : 8 * c + 9, :]
-
-        def run(body, count):
-            def step(c, carry):
-                body(c)
+
+    def fill(dst, s):
+        @pl.when(s < 4)
+        def _():
+            def one(k, carry):
+                dst[k, 8:10, :] = inner_ref[s - 1, k, 0:2, :]
                 return carry
 
-            lax.fori_loop(0, lax.shift_right_logical(count - 2 * s, 3), step, 0)
-
-        run(lambda c: node_pass(src, c), 31)
-        scale = (0.5 if second else 1.0) * STEP / WEIGHTS[1]
-        run(lambda c: face_pass(src, c, scale), 30)
-        run(lambda c: update_pass(src, dst, c, second), 29)
+            lax.fori_loop(0, 64, one, 0, unroll=16)
+
+        @pl.when(s == 4)
+        def _():
+            def one(k, carry):
+                dst[k, 8:16, :] = strip_ref[k]
+                return carry
+
+            lax.fori_loop(0, 64, one, 0, unroll=16)
 
     def time_step(t, carry):
-        stage(base, mid, 2 * t, False)
-        stage(mid, base, 2 * t + 1, True)
+        for second in (False, True):
+            s = 2 * t + (2 if second else 1)
+            src, dst = (mid, base) if second else (base, mid)
+            blend_at = lambda c, s=s: blend_ref[pl.ds(8 * c + s, 8), :]
+            updates = jnp.where((s > 4) & (s < 8), 2, 1)
+            stage(src, dst, (prim, faces), second, False, 2, blend_at, updates)
+            fill(dst, s)
         return carry
 
     lax.fori_loop(0, FSTEPS, time_step, 0)
@@ -255,7 +326,7 @@
     later = jnp.where(slab_ref[0] == 0, 0.0, 1.0).astype(jnp.float32)
     for v in range(4):
         factor = factor_ref[v]
-        mean = weighted_mean([own_ref[v * 16 + n] for n in range(16)])
+        mean = weighted_mean([own_ref[v * 16 + n, :, :] for n in range(16)])
         for i in range(4):
             kept = []
             for j in range(4):
@@ -337,6 +408,17 @@
     return pltpu.with_memory_space_constraint(x, pltpu.VMEM)
 
 
+def work(count):
+    shapes = [(64, count, 128), (64, count, 128), (7 * 16, count, 128), (16, count, 128)]
+    return [pltpu.VMEM(shape, jnp.float32) for shape in shapes]
+
+
+def estimate(updates):
+    return pl.CostEstimate(
+        flops=updates * 400_000_000, transcendentals=0, bytes_accessed=updates * 1_000_000
+    )
+
+
 def ring(axis, shift):
     count = lax.axis_size(axis)
     return [(i, (i + shift) % count) for i in range(count)]
@@ -351,23 +433,37 @@
     own = jnp.concatenate([opening, blend_weight[None], blend_flags[None].astype(f32)], axis=0)
     left = lax.ppermute(own, SPACE, ring(SPACE, 1))
     right = lax.ppermute(own, SPACE, ring(SPACE, -1))
+    own, left, right = hold(own), hold(left), hold(right)
+    inner = pl.pallas_call(
+        inner_kernel,
+        out_shape=pltpu.VMEM((3, 64, 8, 128), f32),
+        in_specs=[vmem],
+        out_specs=vmem,
+        scratch_shapes=work(16),
+        cost_estimate=estimate(3),
+        name="inner",
+    )(own)
+    strip = pl.pallas_call(
+        right_kernel,
+        out_shape=pltpu.VMEM((64, 8, 128), f32),
+        in_specs=[vmem] * 3,
+        out_specs=vmem,
+        scratch_shapes=work(24) + [pltpu.VMEM((24, 128), f32)],
+        cost_estimate=estimate(4),
+        name="right",
+    )(own, right, hold(inner))
     packed, plain = pl.pallas_call(
         fine_kernel,
         out_shape=(
             pltpu.VMEM((16, 4, 8, 128), f32),
             pltpu.VMEM((64, 8, 128), f32),
         ),
-        in_specs=[smem] + [vmem] * 4,
+        in_specs=[smem] + [vmem] * 6,
         out_specs=[vmem] * 2,
-        scratch_shapes=[
-            pltpu.VMEM((64, ROWS, 128), f32),
-            pltpu.VMEM((64, ROWS, 128), f32),
-            pltpu.VMEM((ROWS, 128), f32),
-            pltpu.VMEM((7 * 16, ROWS, 128), f32),
-            pltpu.VMEM((16, ROWS, 128), f32),
-        ],
+        scratch_shapes=work(24) + [pltpu.VMEM((24, 128), f32)],
+        cost_estimate=estimate(11),
         name="fine",
-    )(slab, hold(own), hold(left), hold(right), coarse_factor)
+    )(slab, own, left, right, hold(inner), hold(strip), coarse_factor)
     gathered = lax.all_to_all(packed, TM, 0, 0)
     scanned = pl.pallas_call(
         scan_kernel,

time: 85.6 us -> 81.4 us (0.951)
  waiting for transfers between devices: 10.4 us -> 4.37 us
  blocking collectives: 45 us -> 47.5 us
    pallas_call x1, Pallas kernels: 16.5 us -> 9.74 us  [on_device(): pl.pallas_call(fine_kernel, out_shape=(pltpu.VMEM((16, 4, 8, 128), f32),...]
    pallas_call x0 -> x2, Pallas kernels: none -> 6.02 us  [the longest x1 3.82 us: on_device(): pl.pallas_call(right_kernel, out_shape=pltpu.VMEM((64, 8, 128), f32), in_...]
    ppermute x1, waiting for transfers between devices: 5.24 us -> 1.41 us  [on_device(): left = lax.ppermute(own, SPACE, ring(SPACE, 1))]
    all_to_all x1, blocking collectives: 8.97 us -> 11.5 us  [on_device(): shared = lax.all_to_all(partial_sums, SPACE, 0, 0)]
    ppermute x1, waiting for transfers between devices: 5.16 us -> 2.96 us  [on_device(): right = lax.ppermute(own, SPACE, ring(SPACE, -1))]
  transfers between devices with their start and end apart: 2 -> 2, of which waited for: 2 -> 2; matrix products, arithmetic and copies ran while one was open for 0% -> 0% of each run, Pallas kernels for 0% -> 7%
where the time goes in v2:
time: 81.4 us; the launch traced here: 80.9 us
  blocking collectives  47.5 us (58%)
  Pallas kernels  18.4 us (23%)
  starting transfers between devices  5.83 us (7%)
  waiting for transfers between devices  4.37 us (5%)
  between operations  2.48 us (3%)
  other arithmetic  2.28 us (3%)
    all_to_all x1, blocking collectives, on_device(): gathered = lax.all_to_all(packed, TM, 0, 0)  21.7 us
    all_to_all x1, blocking collectives, on_device(): starts = lax.all_to_all(scanned, TM, 0, 0)  14.4 us
    all_to_all x1, blocking collectives, on_device(): shared = lax.all_to_all(partial_sums, SPACE, 0, 0)  11.5 us
    pallas_call x1, Pallas kernels, on_device(): pl.pallas_call(fine_kernel, out_shape=(pltpu.VMEM((16, 4, 8, 128), f32),...  9.74 us
    ppermute x1, starting transfers between devices, on_device(): right = lax.ppermute(own, SPACE, ring(SPACE, -1))  5.82 us
    pallas_call x1, Pallas kernels, on_device(): pl.pallas_call(right_kernel, out_shape=pltpu.VMEM((64, 8, 128), f32), in_...  3.82 us
    ppermute x1, waiting for transfers between devices, on_device(): right = lax.ppermute(own, SPACE, ring(SPACE, -1))  2.96 us
    pallas_call x1, Pallas kernels, on_device(): pl.pallas_call(inner_kernel, out_shape=pltpu.VMEM((3, 64, 8, 128), f32),...  2.19 us
  transfers between devices with their start and end apart: 2, of which 2 were waited for; matrix products, arithmetic and copies ran while one was open for 0% of the time, Pallas kernels for 7%

profile of v2, /device:TPU:1, one launch (start us, length us, event | category | flops | bytes accessed | tf_op | source)
XLA Modules:
  0.0 80.9 jit_solution(4402274625098559621)
XLA Ops:
  0.6 0.0 copy-start
  0.6 0.7 convert_bitcast_fusion
  1.3 0.0 copy-done
  1.3 1.0 %pad_maximum_fusion.own_ref = f32[66,8,128]{2,1,0:T(8,128)S(1)} fusion(f32[1,8,128]{2,1,0:T(8,128)S(1)} %convert_bitcast_fusion, f32[1,8,128]{2,1,0:T(8,128)S(1)} %bitcast.9, f32[64,8,128]{2,1,0:T(8,128)} %bitcast.7), kind=kLoop, calls=%fused_computation | loop fusion | flops 135168 | bytes 540672 | tf_op jit(solution)/shard_map/concatenate | solution.py:433
  2.3 5.8 %collective-permute-start.1 = (f32[66,8,128]{2,1,0:T(8,128)S(1)}, f32[66,8,128]{2,1,0:T(8,128)S(1)}, u32[]{:S(2)}, u32[]{:S(2)}) collective-permute-start(f32[66,8,128]{2,1,0:T(8,128)S(1)} %pad_maximum_fusion.own_ref), channel_id=1, source_target_pairs={{0,15},{1,0},{2,1},{3,2},{4,3},{5,4},{6,5},{7,6},{8,7},{9,8},{10,9... | collective-permute-start | bytes 811016 | tf_op jit(solution)/shard_map/ppermute | solution.py:435
  8.1 0.0 collective-permute-start
  8.1 2.2 %inner.1.inner_ref = f32[3,64,8,128]{3,2,1,0:T(8,128)S(1)} custom-call(f32[66,8,128]{2,1,0:T(8,128)S(1)} %pad_maximum_fusion.own_ref), custom_call_target="tpu_custom_call" | custom-call | flops 1200000000 | bytes 3000000 | tf_op jit(solution)/shard_map/inner/pallas_call | solution.py:437
  10.3 3.0 %collective-permute-done.1.right_ref = f32[66,8,128]{2,1,0:T(8,128)S(1)} collective-permute-done((f32[66,8,128]{2,1,0:T(8,128)S(1)}, f32[66,8,128]{2,1,0:T(8,128)S(1)}, u32[]{:S(2)}, u32[]{:S(2)}) %collective-permute-start.1) | collective-permute-done | bytes 270368 | tf_op jit(solution)/shard_map/ppermute | solution.py:435
  13.3 3.8 %right.1.strip_ref = f32[64,8,128]{2,1,0:T(8,128)S(1)} custom-call(f32[66,8,128]{2,1,0:T(8,128)S(1)} %pad_maximum_fusion.own_ref, f32[66,8,128]{2,1,0:T(8,128)S(1)} %collective-permute-done.1.right_ref, f32[3,64,8,128]{3,2,1,0:T(8,128)S(1)} %inner.1.inner_ref), custom_call_target="tpu_custom_call" | custom-call | flops 1600000000 | bytes 4000000 | tf_op jit(solution)/shard_map/right/pallas_call | solution.py:446
  17.1 1.4 %collective-permute-done.left_ref = f32[66,8,128]{2,1,0:T(8,128)S(1)} collective-permute-done((f32[66,8,128]{2,1,0:T(8,128)S(1)}, f32[66,8,128]{2,1,0:T(8,128)S(1)}, u32[]{:S(2)}, u32[]{:S(2)}) %collective-permute-start) | collective-permute-done | bytes 270368 | tf_op jit(solution)/shard_map/ppermute | solution.py:434
  18.5 9.7 %fine.1 = (f32[16,4,8,128]{3,2,1,0:T(8,128)S(1)}, f32[64,8,128]{2,1,0:T(8,128)S(1)}) custom-call(s32[1]{0:T(128)} %bitcast.slab_ref, f32[66,8,128]{2,1,0:T(8,128)S(1)} %pad_maximum_fusion.own_ref, f32[66,8,128]{2,1,0:T(8,128)S(1)} %collective-permute-done.left_ref, f32[66,8,128]{2,1,0:T(8,128)S(1)} %collective-permute-done.1.right_ref, ...), custom_call_target="tpu_custom_call" | custom-call | flops 4400000000 | bytes 11000000 | tf_op jit(solution)/shard_map/fine/pallas_call | solution.py:455
  28.3 21.7 %all_to_all.15.given_ref = f32[16,4,8,128]{3,2,1,0:T(8,128)S(1)} all-to-all(f32[16,4,8,128]{3,2,1,0:T(8,128)S(1)} %get-tuple-element.6), channel_id=1, replica_groups=mesh['tm_0'=8,'tm_1'=2,'space_0'=4,'space_1'=4] {'tm_0','tm_1'}, dimensions={0} | all-to-all | bytes 524288 | tf_op jit(solution)/shard_map/all_to_all | solution.py:467
  50.0 0.9 %scan.1 = f32[16,4,8,128]{3,2,1,0:T(8,128)S(1)} custom-call(s32[1]{0:T(128)} %bitcast.slab_ref, f32[16,4,8,128]{3,2,1,0:T(8,128)S(1)} %all_to_all.15.given_ref, f32[4,8,128]{2,1,0:T(8,128)} %factor_ref.5), custom_call_target="tpu_custom_call" | custom-call | tf_op jit(solution)/shard_map/scan/pallas_call | solution.py:468
  50.8 14.4 %all_to_all.16.pieces_ref = f32[16,4,8,128]{3,2,1,0:T(8,128)S(1)} all-to-all(f32[16,4,8,128]{3,2,1,0:T(8,128)S(1)} %scan.1), channel_id=1, replica_groups=mesh['tm_0'=8,'tm_1'=2,'space_0'=4,'space_1'=4] {'tm_0','tm_1'}, dimensions={0} | all-to-all | bytes 524288 | tf_op jit(solution)/shard_map/all_to_all | solution.py:475
  65.2 1.8 %final.1 = (f32[64,8,128]{2,1,0:T(8,128)}, f32[16,1,128]{2,1,0:T(1,128)S(1)}) custom-call(s32[1]{0:T(128)} %bitcast.slab_ref, f32[16,4,8,128]{3,2,1,0:T(8,128)S(1)} %all_to_all.16.pieces_ref, f32[64,8,128]{2,1,0:T(8,128)} %bitcast.8, f32[64,8,128]{2,1,0:T(8,128)S(1)} %get-tuple-element.7.plain_ref, f32[4,8,128]{2,1,0:T(8,128)} %factor_ref.5), custom_call_target="tpu_custom_call" | custom-call | tf_op jit(solution)/shard_map/final/pallas_call | solution.py:476
  67.0 11.5 %all_to_all.17 = f32[16,1,128]{2,1,0:T(1,128)S(1)} all-to-all(f32[16,1,128]{2,1,0:T(1,128)S(1)} %get-tuple-element.9), channel_id=1, replica_groups=mesh['tm_0'=8,'tm_1'=2,'space_0'=4,'space_1'=4] {'space_0','space_1'}, dimensions={0} | all-to-all | bytes 16384 | tf_op jit(solution)/shard_map/all_to_all | solution.py:486
  78.5 0.6 slice_reduce_fusion
Async XLA Ops:
  0.6 0.7 copy-start
  2.3 11.0 %collective-permute-start.1 = (f32[66,8,128]{2,1,0:T(8,128)S(1)}, f32[66,8,128]{2,1,0:T(8,128)S(1)}, u32[]{:S(2)}, u32[]{:S(2)}) collective-permute-start(f32[66,8,128]{2,1,0:T(8,128)S(1)} %pad_maximum_fusion.own_ref), channel_id=1, source_target_pairs={{0,15},{1,0},{2,1},{3,2},{4,3},{5,4},{6,5},{7,6},{8,7},{9,8},{10,9... | collective-permute-start | bytes 811016 | tf_op jit(solution)/shard_map/ppermute | solution.py:435
  8.1 10.4 %collective-permute-start = (f32[66,8,128]{2,1,0:T(8,128)S(1)}, f32[66,8,128]{2,1,0:T(8,128)S(1)}, u32[]{:S(2)}, u32[]{:S(2)}) collective-permute-start(f32[66,8,128]{2,1,0:T(8,128)S(1)} %pad_maximum_fusion.own_ref), channel_id=1, source_target_pairs={{0,1},{1,2},{2,3},{3,4},{4,5},{5,6},{6,7},{7,8},{8,9},{9,10},{10,1... | collective-permute-start | bytes 811016 | tf_op jit(solution)/shard_map/ppermute | solution.py:434

commit v3 on v2

--- a/solution.py
+++ b/solution.py
@@ -242,10 +242,24 @@
     )
 
 
+def join_kernel(opening_ref, weight_ref, flags_ref, own_ref, weight, flags, sems):
+    copies = [
+        pltpu.make_async_copy(opening_ref, own_ref.at[pl.ds(0, 64)], sems.at[0]),
+        pltpu.make_async_copy(weight_ref, weight, sems.at[1]),
+        pltpu.make_async_copy(flags_ref, flags, sems.at[2]),
+    ]
+    for copy in copies:
+        copy.start()
+    copies[1].wait()
+    copies[2].wait()
+    own_ref[64] = flags[...].astype(jnp.float32) * weight[...]
+    copies[0].wait()
+
+
 def inner_kernel(own_ref, inner_ref, base, mid, prim, faces):
     for k in range(64):
         base[k, 0:8, :] = own_ref[k]
-    blend = own_ref[64] * own_ref[65]
+    blend = own_ref[64]
     for s in range(1, 4):
         second = s == 2
         src, dst = (mid, base) if second else (base, mid)
@@ -259,8 +273,8 @@
     for k in range(64):
         base[k, 0:2, :] = own_ref[k, 6:8, :]
         base[k, 2:10, :] = right_ref[k]
-    blend_ref[0:8, :] = own_ref[64] * own_ref[65]
-    blend_ref[8:16, :] = right_ref[64] * right_ref[65]
+    blend_ref[0:8, :] = own_ref[64]
+    blend_ref[8:16, :] = right_ref[64]
 
     def fill(dst, s):
         def one(k, carry):
@@ -290,9 +304,9 @@
     for k in range(64):
         base[k, 0:8, :] = left_ref[k]
         base[k, 8:10, :] = own_ref[k, 0:2, :]
-    blend_ref[0:8, :] = left_ref[64] * left_ref[65]
-    blend_ref[8:16, :] = own_ref[64] * own_ref[65]
-    blend_ref[16:24, :] = right_ref[64] * right_ref[65]
+    blend_ref[0:8, :] = left_ref[64]
+    blend_ref[8:16, :] = own_ref[64]
+    blend_ref[16:24, :] = right_ref[64]
 
     def fill(dst, s):
         @pl.when(s < 4)
@@ -430,7 +444,20 @@
     smem = pl.BlockSpec(memory_space=pltpu.SMEM)
     opening = slab_starts.reshape(64, 8, 128)
     slab = lax.axis_index(TM).astype(jnp.int32).reshape(1)
-    own = jnp.concatenate([opening, blend_weight[None], blend_flags[None].astype(f32)], axis=0)
+    raw = pl.BlockSpec(memory_space=pl.ANY)
+    own = pl.pallas_call(
+        join_kernel,
+        out_shape=pltpu.VMEM((65, 8, 128), f32),
+        in_specs=[raw] * 3,
+        out_specs=vmem,
+        scratch_shapes=[
+            pltpu.VMEM((8, 128), f32),
+            pltpu.VMEM((8, 128), jnp.int32),
+            pltpu.SemaphoreType.DMA((3,)),
+        ],
+        name="join",
+    )(opening, blend_weight, blend_flags)
+    factor = hold(coarse_factor)
     left = lax.ppermute(own, SPACE, ring(SPACE, 1))
     right = lax.ppermute(own, SPACE, ring(SPACE, -1))
     own, left, right = hold(own), hold(left), hold(right)
@@ -463,7 +490,7 @@
         scratch_shapes=work(24) + [pltpu.VMEM((24, 128), f32)],
         cost_estimate=estimate(11),
         name="fine",
-    )(slab, own, left, right, hold(inner), hold(strip), coarse_factor)
+    )(slab, own, left, right, hold(inner), hold(strip), factor)
     gathered = lax.all_to_all(packed, TM, 0, 0)
     scanned = pl.pallas_call(
         scan_kernel,
@@ -471,18 +498,18 @@
         in_specs=[smem] + [vmem] * 2,
         out_specs=vmem,
         name="scan",
-    )(slab, hold(gathered), coarse_factor)
+    )(slab, hold(gathered), factor)
     starts = lax.all_to_all(scanned, TM, 0, 0)
     slab_end, partial_sums = pl.pallas_call(
         final_kernel,
         out_shape=(
-            jax.ShapeDtypeStruct((64, 8, 128), f32),
+            pltpu.VMEM((64, 8, 128), f32),
             pltpu.VMEM((16, 1, 128), f32),
         ),
         in_specs=[smem] + [vmem] * 4,
         out_specs=[vmem] * 2,
         name="final",
-    )(slab, hold(starts), opening, hold(plain), coarse_factor)
+    )(slab, hold(starts), own, hold(plain), factor)
     shared = lax.all_to_all(partial_sums, SPACE, 0, 0)
     element_count = lax.axis_size(SPACE) * slab_starts.shape[4] * slab_starts.shape[5]
     jump_norm = jnp.sqrt(jnp.sum(shared[:, 0, 0]) / element_count)

time: 81.4 us -> 78.3 us (0.962)
  blocking collectives: 47.5 us -> 36 us
  waiting for transfers between devices: 4.37 us -> 9.95 us
  starting transfers between devices: 5.83 us -> 11.1 us
  other arithmetic: 2.28 us -> 0.62 us
  Pallas kernels: 18.4 us -> 17.1 us
    all_to_all x1 -> x0, blocking collectives: 11.5 us -> none  [on_device(): shared = lax.all_to_all(partial_sums, SPACE, 0, 0)]
    all_to_all x0 -> x1, waiting for transfers between devices: none -> 5.73 us  [on_device(): shared = lax.all_to_all(partial_sums, SPACE, 0, 0)]
    all_to_all x0 -> x1, starting transfers between devices: none -> 5.27 us  [on_device(): shared = lax.all_to_all(partial_sums, SPACE, 0, 0)]
    concatenate x1 -> x0, other arithmetic: 0.97 us -> none  [on_device(): jnp.concatenate([opening, blend_weight[None], blend_flags[None].astype(f3...]
    pallas_call x1 -> x2, Pallas kernels: 1.81 us -> 1.86 us  [the longest x1 0.98 us: on_device(): pl.pallas_call(join_kernel, out_shape=pltpu.VMEM((65, 8, 128), f32), in_s...]
  transfers between devices with their start and end apart: 2 -> 3, of which waited for: 2 -> 3; matrix products, arithmetic and copies ran while one was open for 0% -> 1% of each run, Pallas kernels for 7% -> 8%
where the time goes in v3:
time: 78.3 us; the launch traced here: 78 us
  blocking collectives  36 us (46%)
  Pallas kernels  17.1 us (22%)
  starting transfers between devices  11.1 us (14%)
  waiting for transfers between devices  9.95 us (13%)
  between operations  2.5 us (3%)
    all_to_all x1, blocking collectives, on_device(): gathered = lax.all_to_all(packed, TM, 0, 0)  21.7 us
    all_to_all x1, blocking collectives, on_device(): starts = lax.all_to_all(scanned, TM, 0, 0)  14.4 us
    pallas_call x1, Pallas kernels, on_device(): pl.pallas_call(fine_kernel, out_shape=(pltpu.VMEM((16, 4, 8, 128), f32),...  9.02 us
    ppermute x1, starting transfers between devices, on_device(): right = lax.ppermute(own, SPACE, ring(SPACE, -1))  5.82 us
    all_to_all x1, waiting for transfers between devices, on_device(): shared = lax.all_to_all(partial_sums, SPACE, 0, 0)  5.73 us
    all_to_all x1, starting transfers between devices, on_device(): shared = lax.all_to_all(partial_sums, SPACE, 0, 0)  5.27 us
    pallas_call x1, Pallas kernels, on_device(): pl.pallas_call(right_kernel, out_shape=pltpu.VMEM((64, 8, 128), f32), in_...  3.85 us
    ppermute x1, waiting for transfers between devices, on_device(): right = lax.ppermute(own, SPACE, ring(SPACE, -1))  2.84 us
  transfers between devices with their start and end apart: 3, of which 3 were waited for; matrix products, arithmetic and copies ran while one was open for 1% of the time, Pallas kernels for 8%

profile of v3, /device:TPU:1, one launch (start us, length us, event | category | flops | bytes accessed | tf_op | source)
XLA Modules:
  0.0 78.0 jit_solution(7697090782892031784)
XLA Ops:
  0.6 1.0 %join.1.own_ref.opening_ref = f32[65,8,128]{2,1,0:T(8,128)S(1)} custom-call(f32[64,8,128]{2,1,0:T(8,128)} %bitcast.5, f32[8,128]{1,0:T(8,128)} %weight_ref.1, s32[8,128]{1,0:T(8,128)} %flags_ref.1), custom_call_target="tpu_custom_call" | custom-call | tf_op jit(solution)/shard_map/join/pallas_call | solution.py:448
  1.6 5.8 %collective-permute-start.1 = (f32[65,8,128]{2,1,0:T(8,128)S(1)}, f32[65,8,128]{2,1,0:T(8,128)S(1)}, u32[]{:S(2)}, u32[]{:S(2)}) collective-permute-start(f32[65,8,128]{2,1,0:T(8,128)S(1)} %join.1.own_ref.opening_ref), channel_id=1, source_target_pairs={{0,15},{1,0},{2,1},{3,2},{4,3},{5,4},{6,5},{7,6},{8,7},{9,8},{10,9... | collective-permute-start | bytes 798728 | tf_op jit(solution)/shard_map/ppermute | solution.py:462
  7.4 0.0 collective-permute-start
  7.4 2.2 %inner.1.inner_ref = f32[3,64,8,128]{3,2,1,0:T(8,128)S(1)} custom-call(f32[65,8,128]{2,1,0:T(8,128)S(1)} %join.1.own_ref.opening_ref), custom_call_target="tpu_custom_call" | custom-call | flops 1200000000 | bytes 3000000 | tf_op jit(solution)/shard_map/inner/pallas_call | solution.py:464
  9.7 0.0 copy-start
  9.7 2.8 %collective-permute-done.1.right_ref = f32[65,8,128]{2,1,0:T(8,128)S(1)} collective-permute-done((f32[65,8,128]{2,1,0:T(8,128)S(1)}, f32[65,8,128]{2,1,0:T(8,128)S(1)}, u32[]{:S(2)}, u32[]{:S(2)}) %collective-permute-start.1) | collective-permute-done | bytes 266272 | tf_op jit(solution)/shard_map/ppermute | solution.py:462
  12.5 3.9 %right.1.strip_ref = f32[64,8,128]{2,1,0:T(8,128)S(1)} custom-call(f32[65,8,128]{2,1,0:T(8,128)S(1)} %join.1.own_ref.opening_ref, f32[65,8,128]{2,1,0:T(8,128)S(1)} %collective-permute-done.1.right_ref, f32[3,64,8,128]{3,2,1,0:T(8,128)S(1)} %inner.1.inner_ref), custom_call_target="tpu_custom_call" | custom-call | flops 1600000000 | bytes 4000000 | tf_op jit(solution)/shard_map/right/pallas_call | solution.py:473
  16.4 1.4 %collective-permute-done.left_ref = f32[65,8,128]{2,1,0:T(8,128)S(1)} collective-permute-done((f32[65,8,128]{2,1,0:T(8,128)S(1)}, f32[65,8,128]{2,1,0:T(8,128)S(1)}, u32[]{:S(2)}, u32[]{:S(2)}) %collective-permute-start) | collective-permute-done | bytes 266272 | tf_op jit(solution)/shard_map/ppermute | solution.py:461
  17.8 0.0 copy-done
  17.8 9.0 %fine.1 = (f32[16,4,8,128]{3,2,1,0:T(8,128)S(1)}, f32[64,8,128]{2,1,0:T(8,128)S(1)}) custom-call(s32[1]{0:T(128)} %bitcast.slab_ref, f32[65,8,128]{2,1,0:T(8,128)S(1)} %join.1.own_ref.opening_ref, f32[65,8,128]{2,1,0:T(8,128)S(1)} %collective-permute-done.left_ref, f32[65,8,128]{2,1,0:T(8,128)S(1)} %collective-permute-done.1.right_ref, ...), custom_call_target="tpu_custom_call" | custom-call | flops 4400000000 | bytes 11000000 | tf_op jit(solution)/shard_map/fine/pallas_call | solution.py:482
  26.8 21.7 %all_to_all.15.given_ref = f32[16,4,8,128]{3,2,1,0:T(8,128)S(1)} all-to-all(f32[16,4,8,128]{3,2,1,0:T(8,128)S(1)} %get-tuple-element.6), channel_id=1, replica_groups=mesh['tm_0'=8,'tm_1'=2,'space_0'=4,'space_1'=4] {'tm_0','tm_1'}, dimensions={0} | all-to-all | bytes 524288 | tf_op jit(solution)/shard_map/all_to_all | solution.py:494
  48.5 0.2 scan.1
  48.6 14.4 %all_to_all.16.pieces_ref = f32[16,4,8,128]{3,2,1,0:T(8,128)S(1)} all-to-all(f32[16,4,8,128]{3,2,1,0:T(8,128)S(1)} %scan.1), channel_id=1, replica_groups=mesh['tm_0'=8,'tm_1'=2,'space_0'=4,'space_1'=4] {'tm_0','tm_1'}, dimensions={0} | all-to-all | bytes 524288 | tf_op jit(solution)/shard_map/all_to_all | solution.py:502
  63.0 0.9 %final.1 = (f32[64,8,128]{2,1,0:T(8,128)S(1)}, f32[16,1,128]{2,1,0:T(1,128)}) custom-call(s32[1]{0:T(128)} %bitcast.slab_ref, f32[16,4,8,128]{3,2,1,0:T(8,128)S(1)} %all_to_all.16.pieces_ref, f32[65,8,128]{2,1,0:T(8,128)S(1)} %join.1.own_ref.opening_ref, f32[64,8,128]{2,1,0:T(8,128)S(1)} %get-tuple-element.7.plain_ref, f32[4,8,128]{2,1,0:T(8,128)S(1)} %copy-done), custom_call_target="tpu_custom_call" | custom-call | tf_op jit(solution)/shard_map/final/pallas_call | solution.py:503
  63.9 5.3 %all-to-all-start.2 = ((f32[16,1,128]{2,1,0:T(1,128)}), f32[16,1,128]{2,1,0:T(1,128)S(1)}, u32[]{:S(2)}, u32[]{:S(2)}) async-start(f32[16,1,128]{2,1,0:T(1,128)} %get-tuple-element.9), calls=%async_computation.2 | async-start | bytes 16384 | tf_op jit(solution)/shard_map/all_to_all | solution.py:513
  69.1 0.7 copy.6
  69.8 5.7 %all-to-all-done.2 = f32[16,1,128]{2,1,0:T(1,128)S(1)} async-done(((f32[16,1,128]{2,1,0:T(1,128)}), f32[16,1,128]{2,1,0:T(1,128)S(1)}, u32[]{:S(2)}, u32[]{:S(2)}) %all-to-all-start.2) | async-done | bytes 8224 | tf_op jit(solution)/shard_map/all_to_all | solution.py:513
  75.6 0.6 slice_reduce_fusion
Async XLA Ops:
  1.6 10.9 %collective-permute-start.1 = (f32[65,8,128]{2,1,0:T(8,128)S(1)}, f32[65,8,128]{2,1,0:T(8,128)S(1)}, u32[]{:S(2)}, u32[]{:S(2)}) collective-permute-start(f32[65,8,128]{2,1,0:T(8,128)S(1)} %join.1.own_ref.opening_ref), channel_id=1, source_target_pairs={{0,15},{1,0},{2,1},{3,2},{4,3},{5,4},{6,5},{7,6},{8,7},{9,8},{10,9... | collective-permute-start | bytes 798728 | tf_op jit(solution)/shard_map/ppermute | solution.py:462
  7.4 10.3 %collective-permute-start = (f32[65,8,128]{2,1,0:T(8,128)S(1)}, f32[65,8,128]{2,1,0:T(8,128)S(1)}, u32[]{:S(2)}, u32[]{:S(2)}) collective-permute-start(f32[65,8,128]{2,1,0:T(8,128)S(1)} %join.1.own_ref.opening_ref), channel_id=1, source_target_pairs={{0,1},{1,2},{2,3},{3,4},{4,5},{5,6},{6,7},{7,8},{8,9},{9,10},{10,1... | collective-permute-start | bytes 798728 | tf_op jit(solution)/shard_map/ppermute | solution.py:461
  9.7 8.1 %copy-start = (f32[4,8,128]{2,1,0:T(8,128)S(1)}, f32[4,8,128]{2,1,0:T(8,128)}, u32[]{:S(2)}) copy-start(f32[4,8,128]{2,1,0:T(8,128)} %factor_ref.5) | copy-start | bytes 49156
  63.9 11.7 %all-to-all-start.2 = ((f32[16,1,128]{2,1,0:T(1,128)}), f32[16,1,128]{2,1,0:T(1,128)S(1)}, u32[]{:S(2)}, u32[]{:S(2)}) async-start(f32[16,1,128]{2,1,0:T(1,128)} %get-tuple-element.9), calls=%async_computation.2 | async-start | bytes 16384 | tf_op jit(solution)/shard_map/all_to_all | solution.py:513

commit v4 on v3

--- a/solution.py
+++ b/solution.py
@@ -299,7 +299,7 @@
 
 def fine_kernel(
     slab_ref, own_ref, left_ref, right_ref, inner_ref, strip_ref, factor_ref,
-    packed_ref, plain_ref, base, mid, prim, faces, blend_ref,
+    sent_ref, plain_ref, base, mid, prim, faces, blend_ref,
 ):
     for k in range(64):
         base[k, 0:8, :] = left_ref[k]
@@ -340,16 +340,14 @@
     later = jnp.where(slab_ref[0] == 0, 0.0, 1.0).astype(jnp.float32)
     for v in range(4):
         factor = factor_ref[v]
-        mean = weighted_mean([own_ref[v * 16 + n, :, :] for n in range(16)])
-        for i in range(4):
-            kept = []
-            for j in range(4):
-                k = at(v, i, j)
-                guess = mean + factor * (own_ref[k] - mean)
-                kept.append(base[k, 0:8, :] - later * guess)
-                plain_ref[k] = kept[j]
-            for q, piece in enumerate(exchange(kept)):
-                packed_ref[v * 4 + q, i] = piece
+        mean = weighted_mean([own_ref[v * 16 + n] for n in range(16)])
+        for n in range(16):
+            k = v * 16 + n
+            guess = mean + factor * (own_ref[k] - mean)
+            plain_ref[k] = base[k, 0:8, :] - later * guess
+    other = 32 * (1 - (slab_ref[0] & 1))
+    for k in range(32):
+        sent_ref[k] = plain_ref[other + k]
 
 
 def weighted_mean(values):
@@ -373,24 +371,48 @@
     return out
 
 
+def chip_parts(slab_ref, plain_ref, got_ref, w):
+    core = slab_ref[0] & 1
+    even_here = core == 0
+    evens, odds = [], []
+    for n in range(16):
+        mine, theirs = plain_ref[32 * core + 16 * w + n], got_ref[16 * w + n]
+        evens.append(jnp.where(even_here, mine, theirs))
+        odds.append(jnp.where(even_here, theirs, mine))
+    return core, evens, odds
+
+
+def pair_kernel(slab_ref, plain_ref, got_ref, factor_ref, out_ref):
+    for w in range(2):
+        core, evens, odds = chip_parts(slab_ref, plain_ref, got_ref, w)
+        factor = factor_ref[2 * core + w]
+        mean = weighted_mean(evens)
+        both = [mean + factor * (x - mean) + y for x, y in zip(evens, odds, strict=True)]
+        for i in range(4):
+            for q, piece in enumerate(exchange(both[4 * i : 4 * i + 4])):
+                out_ref[w * 4 + q, i] = piece
+
+
 def scan_kernel(slab_ref, given_ref, factor_ref, out_ref):
     slab = slab_ref[0]
-    var = lax.shift_right_logical(slab, 2)
-    first = 2 * (slab & 3)
+    chip = lax.shift_right_logical(slab, 1)
+    var = 2 * (slab & 1) + lax.shift_right_logical(chip, 2)
+    first = 2 * (chip & 3)
     row = lax.broadcasted_iota(jnp.int32, (8, 128), 0)
     even = jnp.broadcast_to(factor_ref[var, pl.ds(first, 1), :], (8, 128))
     odd = jnp.broadcast_to(factor_ref[var, pl.ds(first + 1, 1), :], (8, 128))
     factor = jnp.where((row & 1) == 0, even, odd)
+    factor = factor * factor
     outer = (row < 2) | (row >= 6)
     low = jnp.where(outer, WEIGHTS[0], WEIGHTS[1]).astype(jnp.float32) * (WEIGHTS[0] / 4.0)
     high = jnp.where(outer, WEIGHTS[0], WEIGHTS[1]).astype(jnp.float32) * (WEIGHTS[1] / 4.0)
     state = [given_ref[0, i] for i in range(4)]
     for i in range(4):
         out_ref[0, i] = state[i]
-    for n in range(1, 16):
+    for n in range(1, 8):
         for i in range(4):
             out_ref[n, i] = state[i]
-        if n == 15:
+        if n == 7:
             break
         part = (state[0] + state[3]) * low + (state[1] + state[2]) * high
         part = part + pltpu.roll(part, 4, 0)
@@ -398,20 +420,39 @@
         state = [mean + factor * (state[i] - mean) + given_ref[n, i] for i in range(4)]
 
 
-def final_kernel(slab_ref, pieces_ref, opening_ref, plain_ref, factor_ref, end_ref, sum_ref):
+def spread_kernel(slab_ref, pieces_ref, plain_ref, got_ref, factor_ref, kept_ref, sent_ref):
+    later = jnp.where(slab_ref[0] < 2, 0.0, 1.0).astype(jnp.float32)
+    for w in range(2):
+        core, evens, _ = chip_parts(slab_ref, plain_ref, got_ref, w)
+        factor = factor_ref[2 * core + w]
+        starts = []
+        for i in range(4):
+            starts += exchange([pieces_ref[w * 4 + q, i] for q in range(4)])
+        mean = weighted_mean(starts)
+        for n in range(16):
+            second = later * (mean + factor * (starts[n] - mean)) + evens[n]
+            kept_ref[16 * w + n] = jnp.where(core == 0, starts[n], second)
+            sent_ref[16 * w + n] = jnp.where(core == 0, second, starts[n])
+
+
+def final_kernel(
+    slab_ref, kept_ref, got_ref, own_ref, plain_ref, factor_ref, end_ref, sum_ref, starts_ref
+):
     later = jnp.where(slab_ref[0] == 0, 0.0, 1.0).astype(jnp.float32)
+    here = 32 * (slab_ref[0] & 1)
+    for k in range(32):
+        starts_ref[here + k] = kept_ref[k]
+        starts_ref[32 - here + k] = got_ref[k]
     total = jnp.zeros((8, 128), jnp.float32)
     for v in range(4):
         factor = factor_ref[v]
-        starts = []
-        for i in range(4):
-            starts += exchange([pieces_ref[v * 4 + q, i] for q in range(4)])
+        starts = [starts_ref[v * 16 + n] for n in range(16)]
         mean = weighted_mean(starts)
         squares = []
         for n in range(16):
             k = v * 16 + n
             end_ref[k] = later * (mean + factor * (starts[n] - mean)) + plain_ref[k]
-            jump = later * (starts[n] - opening_ref[k])
+            jump = later * (starts[n] - own_ref[k])
             squares.append(jump * jump)
         total = total + weighted_mean(squares)
     total = jnp.sum(total, axis=(0, 1), keepdims=True)
@@ -479,10 +520,10 @@
         cost_estimate=estimate(4),
         name="right",
     )(own, right, hold(inner))
-    packed, plain = pl.pallas_call(
+    sent, plain = pl.pallas_call(
         fine_kernel,
         out_shape=(
-            pltpu.VMEM((16, 4, 8, 128), f32),
+            pltpu.VMEM((32, 8, 128), f32),
             pltpu.VMEM((64, 8, 128), f32),
         ),
         in_specs=[smem] + [vmem] * 6,
@@ -491,25 +532,43 @@
         cost_estimate=estimate(11),
         name="fine",
     )(slab, own, left, right, hold(inner), hold(strip), factor)
-    gathered = lax.all_to_all(packed, TM, 0, 0)
+    plain = hold(plain)
+    got = hold(lax.ppermute(sent, TM[1], ring(TM[1], 1)))
+    both = pl.pallas_call(
+        pair_kernel,
+        out_shape=pltpu.VMEM((8, 4, 8, 128), f32),
+        in_specs=[smem] + [vmem] * 3,
+        out_specs=vmem,
+        name="pair",
+    )(slab, plain, got, factor)
+    gathered = lax.all_to_all(both, TM[0], 0, 0)
     scanned = pl.pallas_call(
         scan_kernel,
-        out_shape=pltpu.VMEM((16, 4, 8, 128), f32),
+        out_shape=pltpu.VMEM((8, 4, 8, 128), f32),
         in_specs=[smem] + [vmem] * 2,
         out_specs=vmem,
         name="scan",
     )(slab, hold(gathered), factor)
-    starts = lax.all_to_all(scanned, TM, 0, 0)
+    pieces = lax.all_to_all(scanned, TM[0], 0, 0)
+    kept, given = pl.pallas_call(
+        spread_kernel,
+        out_shape=(pltpu.VMEM((32, 8, 128), f32), pltpu.VMEM((32, 8, 128), f32)),
+        in_specs=[smem] + [vmem] * 4,
+        out_specs=[vmem] * 2,
+        name="spread",
+    )(slab, hold(pieces), plain, got, factor)
+    arrived = lax.ppermute(given, TM[1], ring(TM[1], 1))
     slab_end, partial_sums = pl.pallas_call(
         final_kernel,
         out_shape=(
             pltpu.VMEM((64, 8, 128), f32),
             pltpu.VMEM((16, 1, 128), f32),
         ),
-        in_specs=[smem] + [vmem] * 4,
+        in_specs=[smem] + [vmem] * 5,
         out_specs=[vmem] * 2,
+        scratch_shapes=[pltpu.VMEM((64, 8, 128), f32)],
         name="final",
-    )(slab, hold(starts), own, hold(plain), factor)
+    )(slab, hold(kept), hold(arrived), own, plain, factor)
     shared = lax.all_to_all(partial_sums, SPACE, 0, 0)
     element_count = lax.axis_size(SPACE) * slab_starts.shape[4] * slab_starts.shape[5]
     jump_norm = jnp.sqrt(jnp.sum(shared[:, 0, 0]) / element_count)

time: 78.3 us -> 75.7 us (0.967)
  blocking collectives: 36 us -> 26.3 us
  starting transfers between devices: 11.1 us -> 16.2 us
  waiting for transfers between devices: 9.95 us -> 11.9 us
    all_to_all x2, blocking collectives: 36 us -> 26.3 us  [the longest x1 15.9 us: on_device(): gathered = lax.all_to_all(both, TM[0], 0, 0)]
    ppermute x0 -> x2, starting transfers between devices: none -> 5.15 us  [the longest x1 3.25 us: on_device(): arrived = lax.ppermute(given, TM[1], ring(TM[1], 1))]
    ppermute x0 -> x2, waiting for transfers between devices: none -> 1.97 us  [the longest x1 0.99 us: on_device(): got = hold(lax.ppermute(sent, TM[1], ring(TM[1], 1)))]
    pallas_call x2 -> x4, Pallas kernels: 9.19 us -> 9.23 us  [the longest x1 8.98 us: on_device(): pl.pallas_call(fine_kernel, out_shape=(pltpu.VMEM((32, 8, 128), f32), plt...]
  transfers between devices with their start and end apart: 3 -> 5, of which waited for: 3 -> 5; matrix products, arithmetic and copies ran while one was open for 1% -> 1% of each run, Pallas kernels for 8% -> 8%
where the time goes in v4:
time: 75.7 us; the launch traced here: 75.5 us
  blocking collectives  26.3 us (35%)
  Pallas kernels  17.2 us (23%)
  starting transfers between devices  16.2 us (21%)
  waiting for transfers between devices  11.9 us (16%)
  between operations  2.51 us (3%)
    all_to_all x1, blocking collectives, on_device(): gathered = lax.all_to_all(both, TM[0], 0, 0)  15.9 us
    all_to_all x1, blocking collectives, on_device(): pieces = lax.all_to_all(scanned, TM[0], 0, 0)  10.4 us
    pallas_call x1, Pallas kernels, on_device(): pl.pallas_call(fine_kernel, out_shape=(pltpu.VMEM((32, 8, 128), f32), plt...  8.98 us
    ppermute x1, starting transfers between devices, on_device(): right = lax.ppermute(own, SPACE, ring(SPACE, -1))  5.82 us
    all_to_all x1, waiting for transfers between devices, on_device(): shared = lax.all_to_all(partial_sums, SPACE, 0, 0)  5.73 us
    all_to_all x1, starting transfers between devices, on_device(): shared = lax.all_to_all(partial_sums, SPACE, 0, 0)  5.27 us
    pallas_call x1, Pallas kernels, on_device(): pl.pallas_call(right_kernel, out_shape=pltpu.VMEM((64, 8, 128), f32), in_...  3.85 us
    ppermute x1, starting transfers between devices, on_device(): arrived = lax.ppermute(given, TM[1], ring(TM[1], 1))  3.25 us
  transfers between devices with their start and end apart: 5, of which 5 were waited for; matrix products, arithmetic and copies ran while one was open for 1% of the time, Pallas kernels for 8%

profile of v4, /device:TPU:1, one launch (start us, length us, event | category | flops | bytes accessed | tf_op | source)
XLA Modules:
  0.0 75.5 jit_solution(5242152986625713395)
XLA Ops:
  0.6 1.0 %join.1.own_ref = f32[65,8,128]{2,1,0:T(8,128)S(1)} custom-call(f32[64,8,128]{2,1,0:T(8,128)} %bitcast.5, f32[8,128]{1,0:T(8,128)} %weight_ref.1, s32[8,128]{1,0:T(8,128)} %flags_ref.1), custom_call_target="tpu_custom_call" | custom-call | tf_op jit(solution)/shard_map/join/pallas_call | solution.py:489
  1.6 5.8 %collective-permute-start.1 = (f32[65,8,128]{2,1,0:T(8,128)S(1)}, f32[65,8,128]{2,1,0:T(8,128)S(1)}, u32[]{:S(2)}, u32[]{:S(2)}) collective-permute-start(f32[65,8,128]{2,1,0:T(8,128)S(1)} %join.1.own_ref), channel_id=1, source_target_pairs={{0,15},{1,0},{2,1},{3,2},{4,3},{5,4},{6,5},{7,6},{8,7},{9,8},{10,9... | collective-permute-start | bytes 798728 | tf_op jit(solution)/shard_map/ppermute | solution.py:503
  7.4 0.0 collective-permute-start
  7.4 2.2 %inner.1.inner_ref = f32[3,64,8,128]{3,2,1,0:T(8,128)S(1)} custom-call(f32[65,8,128]{2,1,0:T(8,128)S(1)} %join.1.own_ref), custom_call_target="tpu_custom_call" | custom-call | flops 1200000000 | bytes 3000000 | tf_op jit(solution)/shard_map/inner/pallas_call | solution.py:505
  9.7 0.0 copy-start
  9.7 2.8 %collective-permute-done.1.right_ref = f32[65,8,128]{2,1,0:T(8,128)S(1)} collective-permute-done((f32[65,8,128]{2,1,0:T(8,128)S(1)}, f32[65,8,128]{2,1,0:T(8,128)S(1)}, u32[]{:S(2)}, u32[]{:S(2)}) %collective-permute-start.1) | collective-permute-done | bytes 266272 | tf_op jit(solution)/shard_map/ppermute | solution.py:503
  12.5 3.9 %right.1.strip_ref = f32[64,8,128]{2,1,0:T(8,128)S(1)} custom-call(f32[65,8,128]{2,1,0:T(8,128)S(1)} %join.1.own_ref, f32[65,8,128]{2,1,0:T(8,128)S(1)} %collective-permute-done.1.right_ref, f32[3,64,8,128]{3,2,1,0:T(8,128)S(1)} %inner.1.inner_ref), custom_call_target="tpu_custom_call" | custom-call | flops 1600000000 | bytes 4000000 | tf_op jit(solution)/shard_map/right/pallas_call | solution.py:514
  16.4 1.4 %collective-permute-done.left_ref = f32[65,8,128]{2,1,0:T(8,128)S(1)} collective-permute-done((f32[65,8,128]{2,1,0:T(8,128)S(1)}, f32[65,8,128]{2,1,0:T(8,128)S(1)}, u32[]{:S(2)}, u32[]{:S(2)}) %collective-permute-start) | collective-permute-done | bytes 266272 | tf_op jit(solution)/shard_map/ppermute | solution.py:502
  17.8 0.0 copy-done
  17.8 9.0 %fine.1 = (f32[32,8,128]{2,1,0:T(8,128)S(1)}, f32[64,8,128]{2,1,0:T(8,128)S(1)}) custom-call(s32[1]{0:T(128)} %bitcast.slab_ref, f32[65,8,128]{2,1,0:T(8,128)S(1)} %join.1.own_ref, f32[65,8,128]{2,1,0:T(8,128)S(1)} %collective-permute-done.left_ref, f32[65,8,128]{2,1,0:T(8,128)S(1)} %collective-permute-done.1.right_ref, ...), custom_call_target="tpu_custom_call" | custom-call | flops 4400000000 | bytes 11000000 | tf_op jit(solution)/shard_map/fine/pallas_call | solution.py:523
  26.7 1.9 %collective-permute-start.2 = (f32[32,8,128]{2,1,0:T(8,128)S(1)}, f32[32,8,128]{2,1,0:T(8,128)S(1)}, u32[]{:S(2)}, u32[]{:S(2)}) collective-permute-start(f32[32,8,128]{2,1,0:T(8,128)S(1)} %get-tuple-element.9), channel_id=1, source_target_pairs={{0,16},{16,0},{1,17},{17,1},{2,18},{18,2},{3,19},{19,3},{4,20},{20... | collective-permute-start | bytes 393224 | tf_op jit(solution)/shard_map/ppermute | solution.py:536
  28.6 1.0 %collective-permute-done.2.got_ref = f32[32,8,128]{2,1,0:T(8,128)S(1)} collective-permute-done((f32[32,8,128]{2,1,0:T(8,128)S(1)}, f32[32,8,128]{2,1,0:T(8,128)S(1)}, u32[]{:S(2)}, u32[]{:S(2)}) %collective-permute-start.2) | collective-permute-done | bytes 131104 | tf_op jit(solution)/shard_map/ppermute | solution.py:536
  29.6 0.1 pair.1
  29.7 15.9 %all_to_all.15.given_ref = f32[8,4,8,128]{3,2,1,0:T(8,128)S(1)} all-to-all(f32[8,4,8,128]{3,2,1,0:T(8,128)S(1)} %pair.1), channel_id=1, replica_groups=mesh['tm_0'=8,'tm_1'=2,'space_0'=4,'space_1'=4] {'tm_0'}, dimensions={0} | all-to-all | bytes 262144 | tf_op jit(solution)/shard_map/all_to_all | solution.py:544
  45.6 0.1 scan.1
  45.7 10.4 %all_to_all.16.pieces_ref = f32[8,4,8,128]{3,2,1,0:T(8,128)S(1)} all-to-all(f32[8,4,8,128]{3,2,1,0:T(8,128)S(1)} %scan.1), channel_id=1, replica_groups=mesh['tm_0'=8,'tm_1'=2,'space_0'=4,'space_1'=4] {'tm_0'}, dimensions={0} | all-to-all | bytes 262144 | tf_op jit(solution)/shard_map/all_to_all | solution.py:552
  56.1 0.1 spread.1
  56.2 3.3 %collective-permute-start.3 = (f32[32,8,128]{2,1,0:T(8,128)S(1)}, f32[32,8,128]{2,1,0:T(8,128)S(1)}, u32[]{:S(2)}, u32[]{:S(2)}) collective-permute-start(f32[32,8,128]{2,1,0:T(8,128)S(1)} %get-tuple-element.11), channel_id=1, source_target_pairs={{0,16},{16,0},{1,17},{17,1},{2,18},{18,2},{3,19},{19,3},{4,20},{20... | collective-permute-start | bytes 393224 | tf_op jit(solution)/shard_map/ppermute | solution.py:560
  59.4 1.0 %collective-permute-done.3.got_ref = f32[32,8,128]{2,1,0:T(8,128)S(1)} collective-permute-done((f32[32,8,128]{2,1,0:T(8,128)S(1)}, f32[32,8,128]{2,1,0:T(8,128)S(1)}, u32[]{:S(2)}, u32[]{:S(2)}) %collective-permute-start.3) | collective-permute-done | bytes 131104 | tf_op jit(solution)/shard_map/ppermute | solution.py:560
  60.4 0.9 %final.1 = (f32[64,8,128]{2,1,0:T(8,128)S(1)}, f32[16,1,128]{2,1,0:T(1,128)}) custom-call(s32[1]{0:T(128)} %bitcast.slab_ref, f32[32,8,128]{2,1,0:T(8,128)S(1)} %get-tuple-element.10.kept_ref, f32[32,8,128]{2,1,0:T(8,128)S(1)} %collective-permute-done.3.got_ref, f32[65,8,128]{2,1,0:T(8,128)S(1)} %join.1.own_ref, ...), custom_call_target="tpu_custom_call" | custom-call | tf_op jit(solution)/shard_map/final/pallas_call | solution.py:561
  61.3 5.3 %all-to-all-start.2 = ((f32[16,1,128]{2,1,0:T(1,128)}), f32[16,1,128]{2,1,0:T(1,128)S(1)}, u32[]{:S(2)}, u32[]{:S(2)}) async-start(f32[16,1,128]{2,1,0:T(1,128)} %get-tuple-element.13), calls=%async_computation.2 | async-start | bytes 16384 | tf_op jit(solution)/shard_map/all_to_all | solution.py:572
  66.6 0.7 copy.6
  67.3 5.7 %all-to-all-done.2 = f32[16,1,128]{2,1,0:T(1,128)S(1)} async-done(((f32[16,1,128]{2,1,0:T(1,128)}), f32[16,1,128]{2,1,0:T(1,128)S(1)}, u32[]{:S(2)}, u32[]{:S(2)}) %all-to-all-start.2) | async-done | bytes 8224 | tf_op jit(solution)/shard_map/all_to_all | solution.py:572
  73.0 0.6 slice_reduce_fusion
Async XLA Ops:
  1.6 10.9 %collective-permute-start.1 = (f32[65,8,128]{2,1,0:T(8,128)S(1)}, f32[65,8,128]{2,1,0:T(8,128)S(1)}, u32[]{:S(2)}, u32[]{:S(2)}) collective-permute-start(f32[65,8,128]{2,1,0:T(8,128)S(1)} %join.1.own_ref), channel_id=1, source_target_pairs={{0,15},{1,0},{2,1},{3,2},{4,3},{5,4},{6,5},{7,6},{8,7},{9,8},{10,9... | collective-permute-start | bytes 798728 | tf_op jit(solution)/shard_map/ppermute | solution.py:503
  7.4 10.3 %collective-permute-start = (f32[65,8,128]{2,1,0:T(8,128)S(1)}, f32[65,8,128]{2,1,0:T(8,128)S(1)}, u32[]{:S(2)}, u32[]{:S(2)}) collective-permute-start(f32[65,8,128]{2,1,0:T(8,128)S(1)} %join.1.own_ref), channel_id=1, source_target_pairs={{0,1},{1,2},{2,3},{3,4},{4,5},{5,6},{6,7},{7,8},{8,9},{9,10},{10,1... | collective-permute-start | bytes 798728 | tf_op jit(solution)/shard_map/ppermute | solution.py:502
  9.7 8.1 %copy-start = (f32[4,8,128]{2,1,0:T(8,128)S(1)}, f32[4,8,128]{2,1,0:T(8,128)}, u32[]{:S(2)}) copy-start(f32[4,8,128]{2,1,0:T(8,128)} %factor_ref.9) | copy-start | bytes 49156
  26.7 2.9 %collective-permute-start.2 = (f32[32,8,128]{2,1,0:T(8,128)S(1)}, f32[32,8,128]{2,1,0:T(8,128)S(1)}, u32[]{:S(2)}, u32[]{:S(2)}) collective-permute-start(f32[32,8,128]{2,1,0:T(8,128)S(1)} %get-tuple-element.9), channel_id=1, source_target_pairs={{0,16},{16,0},{1,17},{17,1},{2,18},{18,2},{3,19},{19,3},{4,20},{20... | collective-permute-start | bytes 393224 | tf_op jit(solution)/shard_map/ppermute | solution.py:536
  56.2 4.2 %collective-permute-start.3 = (f32[32,8,128]{2,1,0:T(8,128)S(1)}, f32[32,8,128]{2,1,0:T(8,128)S(1)}, u32[]{:S(2)}, u32[]{:S(2)}) collective-permute-start(f32[32,8,128]{2,1,0:T(8,128)S(1)} %get-tuple-element.11), channel_id=1, source_target_pairs={{0,16},{16,0},{1,17},{17,1},{2,18},{18,2},{3,19},{19,3},{4,20},{20... | collective-permute-start | bytes 393224 | tf_op jit(solution)/shard_map/ppermute | solution.py:560
  61.3 11.7 %all-to-all-start.2 = ((f32[16,1,128]{2,1,0:T(1,128)}), f32[16,1,128]{2,1,0:T(1,128)S(1)}, u32[]{:S(2)}, u32[]{:S(2)}) async-start(f32[16,1,128]{2,1,0:T(1,128)} %get-tuple-element.13), calls=%async_computation.2 | async-start | bytes 16384 | tf_op jit(solution)/shard_map/all_to_all | solution.py:572

commit v5 on v4

--- a/solution.py
+++ b/solution.py
@@ -12,6 +12,7 @@
 FSTEPS = 4
 SPACE = ("space_0", "space_1")
 TM = ("tm_0", "tm_1")
+PLANE = ("tm_1", "space_0", "space_1")
 STEP = 0.003
 WEIGHTS = (1.0 / 6.0, 5.0 / 6.0, 5.0 / 6.0, 1.0 / 6.0)
 
@@ -180,9 +181,9 @@
             faces[j * 4 + v, rows(c, 0), :] = flux[v]
 
 
-def update_pass(src, dst, prim, faces, c, blend, second, right):
+def update_pass(src, dst, prim, faces, c, blend, second, side):
     here = rows(c, 1)
-    there, start_rows = (rows(c, 2), rows(c, 0)) if right else (rows(c, 0), rows(c, 2))
+    there, start_rows = rows(c, 2 * side), rows(c, 2 - 2 * side)
     scale = (0.5 if second else 1.0) * STEP / WEIGHTS[1]
     sub_share = scale * blend
     split_share = (scale - sub_share) * EDGE
@@ -232,13 +233,13 @@
     lax.fori_loop(0, count, step, 0)
 
 
-def stage(src, dst, work, second, right, chunks, blend_at, updates):
+def stage(src, dst, work, second, side, chunks, blend_at, updates):
     prim, faces = work
     scale = (0.5 if second else 1.0) * STEP / WEIGHTS[1]
     loop(chunks, lambda c: node_pass(src, prim, c))
     loop(chunks, lambda c: face_pass(src, prim, faces, c, scale))
     loop(
-        updates, lambda c: update_pass(src, dst, prim, faces, c, blend_at(c), second, right)
+        updates, lambda c: update_pass(src, dst, prim, faces, c, blend_at(c), second, side)
     )
 
 
@@ -264,74 +265,82 @@
         second = s == 2
         src, dst = (mid, base) if second else (base, mid)
         shifted = pltpu.roll(blend, 8 - s, 0)
-        stage(src, dst, (prim, faces), second, False, 1, lambda c: shifted, 1)
+        stage(src, dst, (prim, faces), second, 0, 1, lambda c: shifted, 1)
         for k in range(64):
             inner_ref[s - 1, k] = dst[k, 0:8, :]
 
 
-def right_kernel(own_ref, right_ref, inner_ref, out_ref, base, mid, prim, faces, blend_ref):
+def begin_strip(base, own_ref, block_ref, side):
     for k in range(64):
-        base[k, 0:2, :] = own_ref[k, 6:8, :]
-        base[k, 2:10, :] = right_ref[k]
-    blend_ref[0:8, :] = own_ref[64]
-    blend_ref[8:16, :] = right_ref[64]
-
-    def fill(dst, s):
-        def one(k, carry):
-            dst[k, 0:2, :] = inner_ref[s - 1, k, pl.ds(6 - 2 * s, 2), :]
-            return carry
-
-        lax.fori_loop(0, 64, one, 0, unroll=16)
+        base[k, pl.ds(2 * side, 8), :] = block_ref[k]
+        base[k, pl.ds(8 - 8 * side, 2), :] = own_ref[k, pl.ds(6 * side, 2), :]
+
+
+def continue_strip(dst, inner_ref, s, side):
+    def one(k, carry):
+        dst[k, pl.ds(8 - 8 * side, 2), :] = inner_ref[s - 1, k, pl.ds(side * (6 - 2 * s), 2), :]
+        return carry
+
+    lax.fori_loop(0, 64, one, 0, unroll=16)
+
+
+def strip_kernel(
+    slab_ref, own_ref, block_ref, inner_ref, out_ref, base, mid, prim, faces, blend_ref
+):
+    side = slab_ref[0] & 1
+    begin_strip(base, own_ref, block_ref, side)
+    blend_ref[0:8, :] = block_ref[64]
+    blend_ref[8:16, :] = own_ref[64]
+    blend_ref[16:24, :] = block_ref[64]
 
     def time_step(t, carry):
         for second in (False, True):
             s = 2 * t + (2 if second else 1)
             src, dst = (mid, base) if second else (base, mid)
-            blend_at = lambda c, s=s: blend_ref[pl.ds(8 - s, 8), :]
-            stage(src, dst, (prim, faces), second, True, 2, blend_at, 1)
-            fill(dst, jnp.minimum(s, 3))
+            blend_at = lambda c, s=s: blend_ref[pl.ds(s + side * (16 - 2 * s), 8), :]
+            stage(src, dst, (prim, faces), second, side, 2, blend_at, 1)
+            continue_strip(dst, inner_ref, jnp.minimum(s, 3), side)
         return carry
 
     lax.fori_loop(0, 2, time_step, 0)
     for k in range(64):
-        out_ref[k] = base[k, 2:10, :]
+        out_ref[k] = base[k, pl.ds(2 * side, 8), :]
 
 
 def fine_kernel(
-    slab_ref, own_ref, left_ref, right_ref, inner_ref, strip_ref, factor_ref,
+    slab_ref, own_ref, first_ref, block_ref, inner_ref, strip_ref, factor_ref,
     sent_ref, plain_ref, base, mid, prim, faces, blend_ref,
 ):
-    for k in range(64):
-        base[k, 0:8, :] = left_ref[k]
-        base[k, 8:10, :] = own_ref[k, 0:2, :]
-    blend_ref[0:8, :] = left_ref[64]
+    other_side = slab_ref[0] & 1
+    side = 1 - other_side
+    begin_strip(base, own_ref, block_ref, side)
+    blend_ref[pl.ds(16 * other_side, 8), :] = first_ref[64]
     blend_ref[8:16, :] = own_ref[64]
-    blend_ref[16:24, :] = right_ref[64]
+    blend_ref[pl.ds(16 * side, 8), :] = block_ref[64]
 
     def fill(dst, s):
         @pl.when(s < 4)
         def _():
-            def one(k, carry):
-                dst[k, 8:10, :] = inner_ref[s - 1, k, 0:2, :]
-                return carry
-
-            lax.fori_loop(0, 64, one, 0, unroll=16)
+            continue_strip(dst, inner_ref, s, side)
 
         @pl.when(s == 4)
         def _():
             def one(k, carry):
-                dst[k, 8:16, :] = strip_ref[k]
+                strip = dst[k, pl.ds(2 * side, 8), :]
+                dst[k, pl.ds(8 * side, 8), :] = strip
+                dst[k, pl.ds(8 - 8 * side, 8), :] = strip_ref[k]
                 return carry
 
             lax.fori_loop(0, 64, one, 0, unroll=16)
 
     def time_step(t, carry):
+        now = jnp.where(t < 2, side, 0)
         for second in (False, True):
             s = 2 * t + (2 if second else 1)
             src, dst = (mid, base) if second else (base, mid)
-            blend_at = lambda c, s=s: blend_ref[pl.ds(8 * c + s, 8), :]
+            blend_at = lambda c, s=s: blend_ref[pl.ds(8 * c + s + now * (16 - 2 * s), 8), :]
             updates = jnp.where((s > 4) & (s < 8), 2, 1)
-            stage(src, dst, (prim, faces), second, False, 2, blend_at, updates)
+            stage(src, dst, (prim, faces), second, now, 2, blend_at, updates)
             fill(dst, s)
         return carry
 
@@ -474,6 +483,15 @@
     )
 
 
+def opposite_rings(shift):
+    count = lax.axis_size(SPACE)
+    return [
+        (core * count + i, core * count + (i + way) % count)
+        for core, way in ((0, shift), (1, -shift))
+        for i in range(count)
+    ]
+
+
 def ring(axis, shift):
     count = lax.axis_size(axis)
     return [(i, (i + shift) % count) for i in range(count)]
@@ -499,9 +517,8 @@
         name="join",
     )(opening, blend_weight, blend_flags)
     factor = hold(coarse_factor)
-    left = lax.ppermute(own, SPACE, ring(SPACE, 1))
-    right = lax.ppermute(own, SPACE, ring(SPACE, -1))
-    own, left, right = hold(own), hold(left), hold(right)
+    own = hold(own)
+    first = hold(lax.ppermute(own, PLANE, opposite_rings(1)))
     inner = pl.pallas_call(
         inner_kernel,
         out_shape=pltpu.VMEM((3, 64, 8, 128), f32),
@@ -511,15 +528,18 @@
         cost_estimate=estimate(3),
         name="inner",
     )(own)
+    again, inner = lax.optimization_barrier((own, inner))
+    block = hold(lax.ppermute(again, PLANE, opposite_rings(-1)))
+    inner = hold(inner)
     strip = pl.pallas_call(
-        right_kernel,
+        strip_kernel,
         out_shape=pltpu.VMEM((64, 8, 128), f32),
-        in_specs=[vmem] * 3,
+        in_specs=[smem] + [vmem] * 3,
         out_specs=vmem,
         scratch_shapes=work(24) + [pltpu.VMEM((24, 128), f32)],
         cost_estimate=estimate(4),
-        name="right",
-    )(own, right, hold(inner))
+        name="strip",
+    )(slab, own, first, inner)
     sent, plain = pl.pallas_call(
         fine_kernel,
         out_shape=(
@@ -531,7 +551,7 @@
         scratch_shapes=work(24) + [pltpu.VMEM((24, 128), f32)],
         cost_estimate=estimate(11),
         name="fine",
-    )(slab, own, left, right, hold(inner), hold(strip), factor)
+    )(slab, own, first, block, inner, hold(strip), factor)
     plain = hold(plain)
     got = hold(lax.ppermute(sent, TM[1], ring(TM[1], 1)))
     both = pl.pallas_call(

time: 75.7 us -> 73.8 us (0.975)
  starting transfers between devices: 16.2 us -> 12.5 us
  Pallas kernels: 17.2 us -> 18 us
    all_to_all x1, starting transfers between devices: 5.27 us -> 3.41 us  [on_device(): shared = lax.all_to_all(partial_sums, SPACE, 0, 0)]
    ppermute x1, starting transfers between devices: 1.9 us -> 0.28 us  [on_device(): got = hold(lax.ppermute(sent, TM[1], ring(TM[1], 1)))]
    pallas_call x1, Pallas kernels: 8.98 us -> 9.86 us  [on_device(): pl.pallas_call(fine_kernel, out_shape=(pltpu.VMEM((32, 8, 128), f32), plt...]
where the time goes in v5:
time: 73.8 us; the launch traced here: 73.5 us
  blocking collectives  26.7 us (36%)
  Pallas kernels  18 us (24%)
  starting transfers between devices  12.5 us (17%)
  waiting for transfers between devices  12.5 us (17%)
  between operations  2.51 us (3%)
    all_to_all x1, blocking collectives, on_device(): gathered = lax.all_to_all(both, TM[0], 0, 0)  16.3 us
    all_to_all x1, blocking collectives, on_device(): pieces = lax.all_to_all(scanned, TM[0], 0, 0)  10.3 us
    pallas_call x1, Pallas kernels, on_device(): pl.pallas_call(fine_kernel, out_shape=(pltpu.VMEM((32, 8, 128), f32), plt...  9.86 us
    ppermute x1, starting transfers between devices, on_device(): first = hold(lax.ppermute(own, PLANE, opposite_rings(1)))  5.82 us
    all_to_all x1, waiting for transfers between devices, on_device(): shared = lax.all_to_all(partial_sums, SPACE, 0, 0)  5.67 us
    pallas_call x1, Pallas kernels, on_device(): pl.pallas_call(strip_kernel, out_shape=pltpu.VMEM((64, 8, 128), f32), in_...  3.85 us
    ppermute x1, waiting for transfers between devices, on_device(): block = hold(lax.ppermute(again, PLANE, opposite_rings(-1)))  3.67 us
    all_to_all x1, starting transfers between devices, on_device(): shared = lax.all_to_all(partial_sums, SPACE, 0, 0)  3.41 us
  transfers between devices with their start and end apart: 5, of which 5 were waited for; matrix products, arithmetic and copies ran while one was open for 1% of the time, Pallas kernels for 8%

profile of v5, /device:TPU:1, one launch (start us, length us, event | category | flops | bytes accessed | tf_op | source)
XLA Modules:
  0.0 73.5 jit_solution(4445073199352956288)
XLA Ops:
  0.6 1.0 %join.1.own_ref = f32[65,8,128]{2,1,0:T(8,128)S(1)} custom-call(f32[64,8,128]{2,1,0:T(8,128)} %bitcast.5, f32[8,128]{1,0:T(8,128)} %weight_ref.1, s32[8,128]{1,0:T(8,128)} %flags_ref.1), custom_call_target="tpu_custom_call" | custom-call | tf_op jit(solution)/shard_map/join/pallas_call | solution.py:507
  1.6 5.8 %collective-permute-start = (f32[65,8,128]{2,1,0:T(8,128)S(1)}, f32[65,8,128]{2,1,0:T(8,128)S(1)}, u32[]{:S(2)}, u32[]{:S(2)}) collective-permute-start(f32[65,8,128]{2,1,0:T(8,128)S(1)} %join.1.own_ref), channel_id=1, source_target_pairs={{0,1},{1,2},{2,3},{3,4},{4,5},{5,6},{6,7},{7,8},{8,9},{9,10},{10,1... | collective-permute-start | bytes 798728 | tf_op jit(solution)/shard_map/ppermute | solution.py:521
  7.4 2.2 %inner.1.inner_ref = f32[3,64,8,128]{3,2,1,0:T(8,128)S(1)} custom-call(f32[65,8,128]{2,1,0:T(8,128)S(1)} %join.1.own_ref), custom_call_target="tpu_custom_call" | custom-call | flops 1200000000 | bytes 3000000 | tf_op jit(solution)/shard_map/inner/pallas_call | solution.py:522
  9.7 0.1 collective-permute-start.1
  9.8 1.0 %collective-permute-done.block_ref.first_ref = f32[65,8,128]{2,1,0:T(8,128)S(1)} collective-permute-done((f32[65,8,128]{2,1,0:T(8,128)S(1)}, f32[65,8,128]{2,1,0:T(8,128)S(1)}, u32[]{:S(2)}, u32[]{:S(2)}) %collective-permute-start) | collective-permute-done | bytes 266272 | tf_op jit(solution)/shard_map/ppermute | solution.py:521
  10.8 0.0 copy-start
  10.8 3.8 %strip.1.strip_ref = f32[64,8,128]{2,1,0:T(8,128)S(1)} custom-call(s32[1]{0:T(128)} %bitcast.slab_ref, f32[65,8,128]{2,1,0:T(8,128)S(1)} %join.1.own_ref, f32[65,8,128]{2,1,0:T(8,128)S(1)} %collective-permute-done.block_ref.first_ref, f32[3,64,8,128]{3,2,1,0:T(8,128)S(1)} %inner.1.inner_ref), custom_call_target="tpu_custom_call" | custom-call | flops 1600000000 | bytes 4000000 | tf_op jit(solution)/shard_map/strip/pallas_call | solution.py:534
  14.7 3.7 %collective-permute-done.1.block_ref = f32[65,8,128]{2,1,0:T(8,128)S(1)} collective-permute-done((f32[65,8,128]{2,1,0:T(8,128)S(1)}, f32[65,8,128]{2,1,0:T(8,128)S(1)}, u32[]{:S(2)}, u32[]{:S(2)}) %collective-permute-start.1) | collective-permute-done | bytes 266272 | tf_op jit(solution)/shard_map/ppermute | solution.py:532
  18.3 0.0 copy-done
  18.3 9.9 %fine.1 = (f32[32,8,128]{2,1,0:T(8,128)S(1)}, f32[64,8,128]{2,1,0:T(8,128)S(1)}) custom-call(s32[1]{0:T(128)} %bitcast.slab_ref, f32[65,8,128]{2,1,0:T(8,128)S(1)} %join.1.own_ref, f32[65,8,128]{2,1,0:T(8,128)S(1)} %collective-permute-done.block_ref.first_ref, f32[65,8,128]{2,1,0:T(8,128)S(1)} %collective-permute-done.1.block_ref, ...), custom_call_target="tpu_custom_call" | custom-call | flops 4400000000 | bytes 11000000 | tf_op jit(solution)/shard_map/fine/pallas_call | solution.py:543
  28.2 0.3 collective-permute-start.2
  28.5 1.2 %collective-permute-done.2.got_ref = f32[32,8,128]{2,1,0:T(8,128)S(1)} collective-permute-done((f32[32,8,128]{2,1,0:T(8,128)S(1)}, f32[32,8,128]{2,1,0:T(8,128)S(1)}, u32[]{:S(2)}, u32[]{:S(2)}) %collective-permute-start.2) | collective-permute-done | bytes 131104 | tf_op jit(solution)/shard_map/ppermute | solution.py:556
  29.6 0.1 pair.1
  29.7 16.3 %all_to_all.15.given_ref = f32[8,4,8,128]{3,2,1,0:T(8,128)S(1)} all-to-all(f32[8,4,8,128]{3,2,1,0:T(8,128)S(1)} %pair.1), channel_id=1, replica_groups=mesh['tm_0'=8,'tm_1'=2,'space_0'=4,'space_1'=4] {'tm_0'}, dimensions={0} | all-to-all | bytes 262144 | tf_op jit(solution)/shard_map/all_to_all | solution.py:564
  46.1 0.1 scan.1
  46.1 10.3 %all_to_all.16.pieces_ref = f32[8,4,8,128]{3,2,1,0:T(8,128)S(1)} all-to-all(f32[8,4,8,128]{3,2,1,0:T(8,128)S(1)} %scan.1), channel_id=1, replica_groups=mesh['tm_0'=8,'tm_1'=2,'space_0'=4,'space_1'=4] {'tm_0'}, dimensions={0} | all-to-all | bytes 262144 | tf_op jit(solution)/shard_map/all_to_all | solution.py:572
  56.5 0.1 spread.1
  56.5 2.9 %collective-permute-start.3 = (f32[32,8,128]{2,1,0:T(8,128)S(1)}, f32[32,8,128]{2,1,0:T(8,128)S(1)}, u32[]{:S(2)}, u32[]{:S(2)}) collective-permute-start(f32[32,8,128]{2,1,0:T(8,128)S(1)} %get-tuple-element.15), channel_id=1, source_target_pairs={{0,16},{16,0},{1,17},{17,1},{2,18},{18,2},{3,19},{19,3},{4,20},{20... | collective-permute-start | bytes 393224 | tf_op jit(solution)/shard_map/ppermute | solution.py:580
  59.4 1.0 %collective-permute-done.3.got_ref = f32[32,8,128]{2,1,0:T(8,128)S(1)} collective-permute-done((f32[32,8,128]{2,1,0:T(8,128)S(1)}, f32[32,8,128]{2,1,0:T(8,128)S(1)}, u32[]{:S(2)}, u32[]{:S(2)}) %collective-permute-start.3) | collective-permute-done | bytes 131104 | tf_op jit(solution)/shard_map/ppermute | solution.py:580
  60.4 0.9 %final.1 = (f32[64,8,128]{2,1,0:T(8,128)S(1)}, f32[16,1,128]{2,1,0:T(1,128)}) custom-call(s32[1]{0:T(128)} %bitcast.slab_ref, f32[32,8,128]{2,1,0:T(8,128)S(1)} %get-tuple-element.14.kept_ref, f32[32,8,128]{2,1,0:T(8,128)S(1)} %collective-permute-done.3.got_ref, f32[65,8,128]{2,1,0:T(8,128)S(1)} %join.1.own_ref, ...), custom_call_target="tpu_custom_call" | custom-call | tf_op jit(solution)/shard_map/final/pallas_call | solution.py:581
  61.3 3.4 %all-to-all-start.2 = ((f32[16,1,128]{2,1,0:T(1,128)}), f32[16,1,128]{2,1,0:T(1,128)S(1)}, u32[]{:S(2)}, u32[]{:S(2)}) async-start(f32[16,1,128]{2,1,0:T(1,128)} %get-tuple-element.17), calls=%async_computation.2 | async-start | bytes 16384 | tf_op jit(solution)/shard_map/all_to_all | solution.py:592
  64.7 0.7 copy.6
  65.4 5.7 %all-to-all-done.2 = f32[16,1,128]{2,1,0:T(1,128)S(1)} async-done(((f32[16,1,128]{2,1,0:T(1,128)}), f32[16,1,128]{2,1,0:T(1,128)S(1)}, u32[]{:S(2)}, u32[]{:S(2)}) %all-to-all-start.2) | async-done | bytes 8224 | tf_op jit(solution)/shard_map/all_to_all | solution.py:592
  71.1 0.6 slice_reduce_fusion
Async XLA Ops:
  1.6 9.2 %collective-permute-start = (f32[65,8,128]{2,1,0:T(8,128)S(1)}, f32[65,8,128]{2,1,0:T(8,128)S(1)}, u32[]{:S(2)}, u32[]{:S(2)}) collective-permute-start(f32[65,8,128]{2,1,0:T(8,128)S(1)} %join.1.own_ref), channel_id=1, source_target_pairs={{0,1},{1,2},{2,3},{3,4},{4,5},{5,6},{6,7},{7,8},{8,9},{9,10},{10,1... | collective-permute-start | bytes 798728 | tf_op jit(solution)/shard_map/ppermute | solution.py:521
  9.7 8.7 %collective-permute-start.1 = (f32[65,8,128]{2,1,0:T(8,128)S(1)}, f32[65,8,128]{2,1,0:T(8,128)S(1)}, u32[]{:S(2)}, u32[]{:S(2)}) collective-permute-start(f32[65,8,128]{2,1,0:T(8,128)S(1)} %join.1.own_ref), channel_id=1, source_target_pairs={{0,15},{1,0},{2,1},{3,2},{4,3},{5,4},{6,5},{7,6},{8,7},{9,8},{10,9... | collective-permute-start | bytes 798728 | tf_op jit(solution)/shard_map/ppermute | solution.py:532
  10.8 7.5 %copy-start = (f32[4,8,128]{2,1,0:T(8,128)S(1)}, f32[4,8,128]{2,1,0:T(8,128)}, u32[]{:S(2)}) copy-start(f32[4,8,128]{2,1,0:T(8,128)} %factor_ref.9) | copy-start | bytes 49156
  28.2 1.4 %collective-permute-start.2 = (f32[32,8,128]{2,1,0:T(8,128)S(1)}, f32[32,8,128]{2,1,0:T(8,128)S(1)}, u32[]{:S(2)}, u32[]{:S(2)}) collective-permute-start(f32[32,8,128]{2,1,0:T(8,128)S(1)} %get-tuple-element.13), channel_id=1, source_target_pairs={{0,16},{16,0},{1,17},{17,1},{2,18},{18,2},{3,19},{19,3},{4,20},{20... | collective-permute-start | bytes 393224 | tf_op jit(solution)/shard_map/ppermute | solution.py:556
  56.5 3.9 %collective-permute-start.3 = (f32[32,8,128]{2,1,0:T(8,128)S(1)}, f32[32,8,128]{2,1,0:T(8,128)S(1)}, u32[]{:S(2)}, u32[]{:S(2)}) collective-permute-start(f32[32,8,128]{2,1,0:T(8,128)S(1)} %get-tuple-element.15), channel_id=1, source_target_pairs={{0,16},{16,0},{1,17},{17,1},{2,18},{18,2},{3,19},{19,3},{4,20},{20... | collective-permute-start | bytes 393224 | tf_op jit(solution)/shard_map/ppermute | solution.py:580
  61.3 9.8 %all-to-all-start.2 = ((f32[16,1,128]{2,1,0:T(1,128)}), f32[16,1,128]{2,1,0:T(1,128)S(1)}, u32[]{:S(2)}, u32[]{:S(2)}) async-start(f32[16,1,128]{2,1,0:T(1,128)} %get-tuple-element.17), calls=%async_computation.2 | async-start | bytes 16384 | tf_op jit(solution)/shard_map/all_to_all | solution.py:592

commit v6 on v5

--- a/solution.py
+++ b/solution.py
@@ -318,33 +318,35 @@
     blend_ref[8:16, :] = own_ref[64]
     blend_ref[pl.ds(16 * side, 8), :] = block_ref[64]
 
-    def fill(dst, s):
-        @pl.when(s < 4)
-        def _():
-            continue_strip(dst, inner_ref, s, side)
-
-        @pl.when(s == 4)
-        def _():
-            def one(k, carry):
-                strip = dst[k, pl.ds(2 * side, 8), :]
-                dst[k, pl.ds(8 * side, 8), :] = strip
-                dst[k, pl.ds(8 - 8 * side, 8), :] = strip_ref[k]
-                return carry
-
-            lax.fori_loop(0, 64, one, 0, unroll=16)
-
-    def time_step(t, carry):
-        now = jnp.where(t < 2, side, 0)
+    def strip_step(t, carry):
         for second in (False, True):
             s = 2 * t + (2 if second else 1)
             src, dst = (mid, base) if second else (base, mid)
-            blend_at = lambda c, s=s: blend_ref[pl.ds(8 * c + s + now * (16 - 2 * s), 8), :]
-            updates = jnp.where((s > 4) & (s < 8), 2, 1)
-            stage(src, dst, (prim, faces), second, now, 2, blend_at, updates)
-            fill(dst, s)
+            blend_at = lambda c, s=s: blend_ref[pl.ds(s + side * (16 - 2 * s), 8), :]
+            stage(src, dst, (prim, faces), second, side, 2, blend_at, 1)
+            continue_strip(dst, inner_ref, jnp.minimum(s, 3), side)
         return carry
 
-    lax.fori_loop(0, FSTEPS, time_step, 0)
+    lax.fori_loop(0, 2, strip_step, 0)
+
+    def merge(k, carry):
+        strip = base[k, pl.ds(2 * side, 8), :]
+        base[k, pl.ds(pl.multiple_of(8 * side, 8), 8), :] = strip
+        base[k, pl.ds(pl.multiple_of(8 - 8 * side, 8), 8), :] = strip_ref[k]
+        return carry
+
+    lax.fori_loop(0, 64, merge, 0, unroll=16)
+
+    def joint_step(t, carry):
+        for second in (False, True):
+            s = 2 * t + (2 if second else 1)
+            src, dst = (mid, base) if second else (base, mid)
+            blend_at = lambda c, s=s: blend_ref[pl.ds(8 * c + s, 8), :]
+            updates = jnp.where(s < 8, 2, 1) if second else 2
+            stage(src, dst, (prim, faces), second, 0, 2, blend_at, updates)
+        return carry
+
+    lax.fori_loop(2, FSTEPS, joint_step, 0)
 
     later = jnp.where(slab_ref[0] == 0, 0.0, 1.0).astype(jnp.float32)
     for v in range(4):

time: 73.8 us -> 73.3 us (level)
  no operation moved by 1% of the time
where the time goes in v6:
time: 73.3 us; the launch traced here: 73 us
  blocking collectives  26.7 us (36%)
  Pallas kernels  17.5 us (24%)
  starting transfers between devices  12.5 us (17%)
  waiting for transfers between devices  12.5 us (17%)
  between operations  2.51 us (3%)
    all_to_all x1, blocking collectives, on_device(): gathered = lax.all_to_all(both, TM[0], 0, 0)  16.3 us
    all_to_all x1, blocking collectives, on_device(): pieces = lax.all_to_all(scanned, TM[0], 0, 0)  10.3 us
    pallas_call x1, Pallas kernels, on_device(): pl.pallas_call(fine_kernel, out_shape=(pltpu.VMEM((32, 8, 128), f32), plt...  9.34 us
    ppermute x1, starting transfers between devices, on_device(): first = hold(lax.ppermute(own, PLANE, opposite_rings(1)))  5.82 us
    all_to_all x1, waiting for transfers between devices, on_device(): shared = lax.all_to_all(partial_sums, SPACE, 0, 0)  5.67 us
    pallas_call x1, Pallas kernels, on_device(): pl.pallas_call(strip_kernel, out_shape=pltpu.VMEM((64, 8, 128), f32), in_...  3.85 us
    ppermute x1, waiting for transfers between devices, on_device(): block = hold(lax.ppermute(again, PLANE, opposite_rings(-1)))  3.67 us
    all_to_all x1, starting transfers between devices, on_device(): shared = lax.all_to_all(partial_sums, SPACE, 0, 0)  3.41 us
  transfers between devices with their start and end apart: 5, of which 5 were waited for; matrix products, arithmetic and copies ran while one was open for 1% of the time, Pallas kernels for 8%

profile of v6, /device:TPU:1, one launch (start us, length us, event | category | flops | bytes accessed | tf_op | source)
XLA Modules:
  0.0 73.0 jit_solution(8358009976631670629)
XLA Ops:
  0.6 1.0 %join.1.own_ref = f32[65,8,128]{2,1,0:T(8,128)S(1)} custom-call(f32[64,8,128]{2,1,0:T(8,128)} %bitcast.5, f32[8,128]{1,0:T(8,128)} %weight_ref.1, s32[8,128]{1,0:T(8,128)} %flags_ref.1), custom_call_target="tpu_custom_call" | custom-call | tf_op jit(solution)/shard_map/join/pallas_call | solution.py:509
  1.6 5.8 %collective-permute-start = (f32[65,8,128]{2,1,0:T(8,128)S(1)}, f32[65,8,128]{2,1,0:T(8,128)S(1)}, u32[]{:S(2)}, u32[]{:S(2)}) collective-permute-start(f32[65,8,128]{2,1,0:T(8,128)S(1)} %join.1.own_ref), channel_id=1, source_target_pairs={{0,1},{1,2},{2,3},{3,4},{4,5},{5,6},{6,7},{7,8},{8,9},{9,10},{10,1... | collective-permute-start | bytes 798728 | tf_op jit(solution)/shard_map/ppermute | solution.py:523
  7.4 2.2 %inner.1.inner_ref = f32[3,64,8,128]{3,2,1,0:T(8,128)S(1)} custom-call(f32[65,8,128]{2,1,0:T(8,128)S(1)} %join.1.own_ref), custom_call_target="tpu_custom_call" | custom-call | flops 1200000000 | bytes 3000000 | tf_op jit(solution)/shard_map/inner/pallas_call | solution.py:524
  9.7 0.1 collective-permute-start.1
  9.8 1.0 %collective-permute-done.block_ref.first_ref = f32[65,8,128]{2,1,0:T(8,128)S(1)} collective-permute-done((f32[65,8,128]{2,1,0:T(8,128)S(1)}, f32[65,8,128]{2,1,0:T(8,128)S(1)}, u32[]{:S(2)}, u32[]{:S(2)}) %collective-permute-start) | collective-permute-done | bytes 266272 | tf_op jit(solution)/shard_map/ppermute | solution.py:523
  10.8 0.0 copy-start
  10.8 3.8 %strip.1.strip_ref = f32[64,8,128]{2,1,0:T(8,128)S(1)} custom-call(s32[1]{0:T(128)} %bitcast.slab_ref, f32[65,8,128]{2,1,0:T(8,128)S(1)} %join.1.own_ref, f32[65,8,128]{2,1,0:T(8,128)S(1)} %collective-permute-done.block_ref.first_ref, f32[3,64,8,128]{3,2,1,0:T(8,128)S(1)} %inner.1.inner_ref), custom_call_target="tpu_custom_call" | custom-call | flops 1600000000 | bytes 4000000 | tf_op jit(solution)/shard_map/strip/pallas_call | solution.py:536
  14.7 3.7 %collective-permute-done.1.block_ref = f32[65,8,128]{2,1,0:T(8,128)S(1)} collective-permute-done((f32[65,8,128]{2,1,0:T(8,128)S(1)}, f32[65,8,128]{2,1,0:T(8,128)S(1)}, u32[]{:S(2)}, u32[]{:S(2)}) %collective-permute-start.1) | collective-permute-done | bytes 266272 | tf_op jit(solution)/shard_map/ppermute | solution.py:534
  18.3 0.0 copy-done
  18.3 9.3 %fine.1 = (f32[32,8,128]{2,1,0:T(8,128)S(1)}, f32[64,8,128]{2,1,0:T(8,128)S(1)}) custom-call(s32[1]{0:T(128)} %bitcast.slab_ref, f32[65,8,128]{2,1,0:T(8,128)S(1)} %join.1.own_ref, f32[65,8,128]{2,1,0:T(8,128)S(1)} %collective-permute-done.block_ref.first_ref, f32[65,8,128]{2,1,0:T(8,128)S(1)} %collective-permute-done.1.block_ref, ...), custom_call_target="tpu_custom_call" | custom-call | flops 4400000000 | bytes 11000000 | tf_op jit(solution)/shard_map/fine/pallas_call | solution.py:545
  27.7 0.3 collective-permute-start.2
  27.9 1.2 %collective-permute-done.2.got_ref = f32[32,8,128]{2,1,0:T(8,128)S(1)} collective-permute-done((f32[32,8,128]{2,1,0:T(8,128)S(1)}, f32[32,8,128]{2,1,0:T(8,128)S(1)}, u32[]{:S(2)}, u32[]{:S(2)}) %collective-permute-start.2) | collective-permute-done | bytes 131104 | tf_op jit(solution)/shard_map/ppermute | solution.py:558
  29.1 0.1 pair.1
  29.2 16.3 %all_to_all.15.given_ref = f32[8,4,8,128]{3,2,1,0:T(8,128)S(1)} all-to-all(f32[8,4,8,128]{3,2,1,0:T(8,128)S(1)} %pair.1), channel_id=1, replica_groups=mesh['tm_0'=8,'tm_1'=2,'space_0'=4,'space_1'=4] {'tm_0'}, dimensions={0} | all-to-all | bytes 262144 | tf_op jit(solution)/shard_map/all_to_all | solution.py:566
  45.5 0.1 scan.1
  45.6 10.3 %all_to_all.16.pieces_ref = f32[8,4,8,128]{3,2,1,0:T(8,128)S(1)} all-to-all(f32[8,4,8,128]{3,2,1,0:T(8,128)S(1)} %scan.1), channel_id=1, replica_groups=mesh['tm_0'=8,'tm_1'=2,'space_0'=4,'space_1'=4] {'tm_0'}, dimensions={0} | all-to-all | bytes 262144 | tf_op jit(solution)/shard_map/all_to_all | solution.py:574
  55.9 0.1 spread.1
  56.0 2.9 %collective-permute-start.3 = (f32[32,8,128]{2,1,0:T(8,128)S(1)}, f32[32,8,128]{2,1,0:T(8,128)S(1)}, u32[]{:S(2)}, u32[]{:S(2)}) collective-permute-start(f32[32,8,128]{2,1,0:T(8,128)S(1)} %get-tuple-element.15), channel_id=1, source_target_pairs={{0,16},{16,0},{1,17},{17,1},{2,18},{18,2},{3,19},{19,3},{4,20},{20... | collective-permute-start | bytes 393224 | tf_op jit(solution)/shard_map/ppermute | solution.py:582
  58.9 1.0 %collective-permute-done.3.got_ref = f32[32,8,128]{2,1,0:T(8,128)S(1)} collective-permute-done((f32[32,8,128]{2,1,0:T(8,128)S(1)}, f32[32,8,128]{2,1,0:T(8,128)S(1)}, u32[]{:S(2)}, u32[]{:S(2)}) %collective-permute-start.3) | collective-permute-done | bytes 131104 | tf_op jit(solution)/shard_map/ppermute | solution.py:582
  59.9 0.9 %final.1 = (f32[64,8,128]{2,1,0:T(8,128)S(1)}, f32[16,1,128]{2,1,0:T(1,128)}) custom-call(s32[1]{0:T(128)} %bitcast.slab_ref, f32[32,8,128]{2,1,0:T(8,128)S(1)} %get-tuple-element.14.kept_ref, f32[32,8,128]{2,1,0:T(8,128)S(1)} %collective-permute-done.3.got_ref, f32[65,8,128]{2,1,0:T(8,128)S(1)} %join.1.own_ref, ...), custom_call_target="tpu_custom_call" | custom-call | tf_op jit(solution)/shard_map/final/pallas_call | solution.py:583
  60.8 3.4 %all-to-all-start.2 = ((f32[16,1,128]{2,1,0:T(1,128)}), f32[16,1,128]{2,1,0:T(1,128)S(1)}, u32[]{:S(2)}, u32[]{:S(2)}) async-start(f32[16,1,128]{2,1,0:T(1,128)} %get-tuple-element.17), calls=%async_computation.2 | async-start | bytes 16384 | tf_op jit(solution)/shard_map/all_to_all | solution.py:594
  64.2 0.7 copy.6
  64.9 5.7 %all-to-all-done.2 = f32[16,1,128]{2,1,0:T(1,128)S(1)} async-done(((f32[16,1,128]{2,1,0:T(1,128)}), f32[16,1,128]{2,1,0:T(1,128)S(1)}, u32[]{:S(2)}, u32[]{:S(2)}) %all-to-all-start.2) | async-done | bytes 8224 | tf_op jit(solution)/shard_map/all_to_all | solution.py:594
  70.6 0.6 slice_reduce_fusion
Async XLA Ops:
  1.6 9.2 %collective-permute-start = (f32[65,8,128]{2,1,0:T(8,128)S(1)}, f32[65,8,128]{2,1,0:T(8,128)S(1)}, u32[]{:S(2)}, u32[]{:S(2)}) collective-permute-start(f32[65,8,128]{2,1,0:T(8,128)S(1)} %join.1.own_ref), channel_id=1, source_target_pairs={{0,1},{1,2},{2,3},{3,4},{4,5},{5,6},{6,7},{7,8},{8,9},{9,10},{10,1... | collective-permute-start | bytes 798728 | tf_op jit(solution)/shard_map/ppermute | solution.py:523
  9.7 8.7 %collective-permute-start.1 = (f32[65,8,128]{2,1,0:T(8,128)S(1)}, f32[65,8,128]{2,1,0:T(8,128)S(1)}, u32[]{:S(2)}, u32[]{:S(2)}) collective-permute-start(f32[65,8,128]{2,1,0:T(8,128)S(1)} %join.1.own_ref), channel_id=1, source_target_pairs={{0,15},{1,0},{2,1},{3,2},{4,3},{5,4},{6,5},{7,6},{8,7},{9,8},{10,9... | collective-permute-start | bytes 798728 | tf_op jit(solution)/shard_map/ppermute | solution.py:534
  10.8 7.5 %copy-start = (f32[4,8,128]{2,1,0:T(8,128)S(1)}, f32[4,8,128]{2,1,0:T(8,128)}, u32[]{:S(2)}) copy-start(f32[4,8,128]{2,1,0:T(8,128)} %factor_ref.9) | copy-start | bytes 49156
  27.7 1.4 %collective-permute-start.2 = (f32[32,8,128]{2,1,0:T(8,128)S(1)}, f32[32,8,128]{2,1,0:T(8,128)S(1)}, u32[]{:S(2)}, u32[]{:S(2)}) collective-permute-start(f32[32,8,128]{2,1,0:T(8,128)S(1)} %get-tuple-element.13), channel_id=1, source_target_pairs={{0,16},{16,0},{1,17},{17,1},{2,18},{18,2},{3,19},{19,3},{4,20},{20... | collective-permute-start | bytes 393224 | tf_op jit(solution)/shard_map/ppermute | solution.py:558
  56.0 3.9 %collective-permute-start.3 = (f32[32,8,128]{2,1,0:T(8,128)S(1)}, f32[32,8,128]{2,1,0:T(8,128)S(1)}, u32[]{:S(2)}, u32[]{:S(2)}) collective-permute-start(f32[32,8,128]{2,1,0:T(8,128)S(1)} %get-tuple-element.15), channel_id=1, source_target_pairs={{0,16},{16,0},{1,17},{17,1},{2,18},{18,2},{3,19},{19,3},{4,20},{20... | collective-permute-start | bytes 393224 | tf_op jit(solution)/shard_map/ppermute | solution.py:582
  60.8 9.8 %all-to-all-start.2 = ((f32[16,1,128]{2,1,0:T(1,128)}), f32[16,1,128]{2,1,0:T(1,128)S(1)}, u32[]{:S(2)}, u32[]{:S(2)}) async-start(f32[16,1,128]{2,1,0:T(1,128)} %get-tuple-element.17), calls=%async_computation.2 | async-start | bytes 16384 | tf_op jit(solution)/shard_map/all_to_all | solution.py:594
